TPU v7x, 32 devices: a whole 2x2x4 slice. The times are simulated.
32 devices in a mesh: tm: 8 (over z, y), rows: 4 (over x, core).
Axes of the slice: x: 2, y: 2, z: 4, core: 2. Of those that a mesh axis runs over, the one named last changes fastest.
Arguments:
- upstream: bfloat16 [32, 32, 128, 128], P('tm', 'rows'), may hold values from -6 to 6
- saved_first: bfloat16 [32, 32, 128, 128], P('tm', 'rows'), may hold values from -8 to 8
- saved_second: bfloat16 [32, 32, 128, 128], P('tm', 'rows'), may hold values from -8 to 8
- weight_first: bfloat16 [3456, 128], replicated, may hold values from -0.109375 to 0.109375
- weight_second: bfloat16 [3456, 128], replicated, may hold values from -0.109375 to 0.109375
Outputs:
- grad_input: bfloat16 [32, 32, 128, 128], P('tm', 'rows')
- wgrad_first: float32 [3456, 128], P('tm')
- wgrad_second: float32 [3456, 128], P('tm')
All inputs are finite; a program needn't handle non-finite values.
Results may differ from a plain program's by a relative error of at most 0.005.
Values may be sent and summed in bfloat16 or wider, within the bound.
A program may use at most 64 MiB of HBM per device.

v0:
```python
import functools
import math

import jax
import jax.numpy as jnp
from jax import lax
from jax.experimental import pallas as pl
from jax.experimental.pallas import tpu as pltpu
from jax.sharding import PartitionSpec as P

F32, BF16 = jnp.float32, jnp.bfloat16
VMEM_LIMIT = 60 * 1024 * 1024


def shifted(block, axis, step):
    count = lax.axis_size(axis)
    route = [(i - step, i) for i in range(count) if 0 <= i - step < count]
    return lax.ppermute(block, axis, route)


def halos(grad):
    height = grad.shape[1]
    above = shifted(grad[:, height - 1 :], "rows", 1)
    below = shifted(grad[:, :1], "rows", -1)
    later = shifted(grad[:2], "tm", -1)
    later_edges = shifted(jnp.concatenate([above[:2], below[:2]], axis=1), "tm", -1)
    return above, below, later, later_edges


def fill_row(cols, value, frame, row, height, width, chans):
    wide = value.astype(F32)
    place = lax.broadcasted_iota(jnp.int32, (width, chans), 0)
    after = jnp.where(place == width - 1, 0.0, pltpu.roll(wide, width - 1, 0)).astype(BF16)
    before = jnp.where(place == 0, 0.0, pltpu.roll(wide, 1, 0)).astype(BF16)
    for q in range(3):
        out_row = row - 1 + q
        if not 0 <= out_row < height:
            continue
        base = (frame * 9 + q * 3) * chans
        lines = pl.ds(out_row * width, width)
        cols[lines, pl.ds(base, chans)] = after
        cols[lines, pl.ds(base + chans, chans)] = value
        cols[lines, pl.ds(base + 2 * chans, chans)] = before


def fill(cols, grad_ref, above_ref, below_ref, later_ref, edges_ref):
    frames, height, width, chans = grad_ref.shape
    put = functools.partial(fill_row, cols, height=height, width=width, chans=chans)
    for frame in range(frames + 2):
        late = frame - frames
        if late < 0:
            first, last = above_ref[frame, 0], below_ref[frame, 0]
        else:
            first, last = edges_ref[late, 0], edges_ref[late, 1]
        put(first, frame, -1)
        put(last, frame, height)
        for row in range(height):
            put(grad_ref[frame, row] if late < 0 else later_ref[late, row], frame, row)


def spread_kernel(grad_ref, above_ref, below_ref, later_ref, edges_ref, saved_ref, weight_ref, out_ref, cols, kernels):
    frames, height, width, chans = grad_ref.shape
    span = 9 * chans
    for half in range(2):
        for j in range(4):
            p = 2 + half - j
            for tap in range(9):
                block = (
                    weight_ref[pl.ds((9 * p + tap) * chans, chans), :]
                    if 0 <= p < 3
                    else jnp.zeros((chans, chans), BF16)
                )
                kernels[pl.ds(half * chans, chans), pl.ds(j * span + tap * chans, chans)] = block
    fill(cols, grad_ref, above_ref, below_ref, later_ref, edges_ref)
    step_rows = math.gcd(4, height)
    lines = step_rows * width
    for pair in range(frames // 2):

        def chunk(index, carry, pair=pair):
            part = cols[pl.ds(pl.multiple_of(index * lines, lines), lines), pl.ds(pair * 2 * span, 4 * span)]
            spread = lax.dot_general(part, kernels[...], (((1,), (1,)), ((), ())), preferred_element_type=F32)
            for half in range(2):
                rows = pl.ds(index * step_rows, step_rows)
                value = saved_ref[2 * pair + half, rows].reshape(lines, chans).astype(F32)
                sigma = jax.nn.sigmoid(value)
                slope = sigma * (1.0 + value * (1.0 - sigma))
                result = spread[:, half * chans : (half + 1) * chans] * slope
                out_ref[2 * pair + half, rows] = result.astype(BF16).reshape(step_rows, width, chans)
            return carry

        lax.fori_loop(0, height // step_rows, chunk, 0)


def wsum_kernel(grad_ref, above_ref, below_ref, later_ref, edges_ref, saved_ref, out_ref, cols, active):
    frames, height, width, chans = grad_ref.shape
    span = 9 * chans
    fill(cols, grad_ref, above_ref, below_ref, later_ref, edges_ref)
    for frame in range(frames):
        for row in range(height):
            value = saved_ref[frame, row].astype(F32)
            act = value * jax.nn.sigmoid(value)
            active[pl.ds(frame * chans, chans), pl.ds(row * width, width)] = act.T.astype(BF16)
    out_ref[...] = jnp.zeros_like(out_ref)
    for frame in range(frames + 2):
        low, high = max(0, frame - 2), min(frames, frame + 1)
        acts = active[pl.ds(low * chans, (high - low) * chans), :]
        for q in range(3):
            part = cols[:, pl.ds(frame * span + q * 3 * chans, 3 * chans)]
            total = jnp.dot(acts, part, preferred_element_type=F32)
            for s in range(low, high):
                p = s + 2 - frame
                for k in range(3):
                    rows = pl.ds((9 * p + 3 * q + k) * chans, chans)
                    out_ref[rows, :] += total[(s - low) * chans : (s - low + 1) * chans, k * chans : (k + 1) * chans]


def vmem(count):
    return [pl.BlockSpec(memory_space=pltpu.VMEM)] * count


def spread_of(pieces, saved, weight):
    frames, height, width, chans = saved.shape
    flops = 2 * frames * height * width * 36 * chans * chans
    return pl.pallas_call(
        spread_kernel,
        out_shape=jax.ShapeDtypeStruct(saved.shape, BF16),
        in_specs=vmem(7),
        out_specs=pl.BlockSpec(memory_space=pltpu.VMEM),
        scratch_shapes=[
            pltpu.VMEM((height * width, (frames + 2) * 9 * chans), BF16),
            pltpu.VMEM((2 * chans, 36 * chans), BF16),
        ],
        compiler_params=pltpu.CompilerParams(vmem_limit_bytes=VMEM_LIMIT),
        cost_estimate=pl.CostEstimate(flops=flops, bytes_accessed=4 * saved.size, transcendentals=0),
        name="spread",
    )(*pieces, saved, weight)


def wsum_of(pieces, saved):
    frames, height, width, chans = saved.shape
    flops = 2 * frames * height * width * 27 * chans * chans
    return pl.pallas_call(
        wsum_kernel,
        out_shape=jax.ShapeDtypeStruct((27 * chans, chans), F32),
        in_specs=vmem(6),
        out_specs=pl.BlockSpec(memory_space=pltpu.VMEM),
        scratch_shapes=[
            pltpu.VMEM((height * width, (frames + 2) * 9 * chans), BF16),
            pltpu.VMEM((frames * chans, height * width), BF16),
        ],
        compiler_params=pltpu.CompilerParams(vmem_limit_bytes=VMEM_LIMIT),
        cost_estimate=pl.CostEstimate(flops=flops, bytes_accessed=4 * saved.size, transcendentals=0),
        name="wsum",
    )(*pieces, saved)


def exchanged_sum(parts, axis, dim):
    return jnp.sum(lax.all_to_all(parts, axis, split_axis=dim, concat_axis=dim, tiled=True), axis=dim)


def reduced(wsum_first, wsum_second, factor):
    depth, chans = wsum_first.shape
    slots, bands = lax.axis_size("tm"), lax.axis_size("rows")
    share = depth // slots
    if share % bands:
        first, second = lax.psum((wsum_first, wsum_second), "rows")
        both = jnp.stack([first.reshape(slots, share, chans), second.reshape(slots, share, chans)], axis=1)
        mine = exchanged_sum(both, "tm", 0) * factor
        return mine[0], mine[1]
    split = (slots, bands, share // bands, chans)
    second = lax.psum_scatter(wsum_second.reshape(split), "rows", scatter_dimension=1, tiled=False)
    first = exchanged_sum(wsum_first.reshape(split), "rows", 1)
    mine = exchanged_sum(jnp.stack([first, second], axis=1), "tm", 0) * factor
    whole = lax.all_gather(mine, "rows", axis=1, tiled=True)
    return whole[0], whole[1]


def body(upstream, saved_first, saved_second, weight_first, weight_second):
    pieces = (upstream, *halos(upstream))
    grad_mid = spread_of(pieces, saved_second, weight_second)
    pieces_mid = (grad_mid, *halos(grad_mid))
    wsum_second = wsum_of(pieces, saved_second)
    grad_input = spread_of(pieces_mid, saved_first, weight_first)
    wsum_first = wsum_of(pieces_mid, saved_first)
    frames, height, width, chans = upstream.shape
    factor = 1.0 / math.sqrt(frames * lax.axis_size("tm") * height * lax.axis_size("rows") * width)
    return (grad_input, *reduced(wsum_first, wsum_second, factor))


def solution(mesh):
    grid = P("tm", "rows", None, None)
    return jax.shard_map(
        body,
        mesh=mesh,
        in_specs=(grid, grid, grid, P(), P()),
        out_specs=(grid, P("tm", None), P("tm", None)),
        check_vma=False,
    )
```

profile of v0, /device:TPU:0, one launch (start us, length us, event | category | flops | bytes accessed | tf_op | source)
XLA Modules:
  0.0 160.6 jit_solution(7852985638606203349)
XLA Ops:
  7.2 1.1 slice.38
  8.3 1.3 collective-permute-start.2
  10.6 1.3 collective-permute-start.1
  11.9 3.0 %collective-permute-start = (bf16[4,1,128,128]{3,2,1,0:T(8,128)(2,1)S(1)}, bf16[4,1,128,128]{3,2,1,0:T(8,128)(2,1)S(1)}, u32[]{:S(2)}, u32[]{:S(2)}) collective-permute-start(bf16[4,1,128,128]{3,2,1,0:T(8,128)(2,1)S(1)} %get-tuple-element.6), channel_id=1, source_target_pairs={{0,1},{1,2},{2,3},{4,5},{5,6},{6,7},{8,9},{9,10},{10,11},{12,13},{... | collective-permute-start | bytes 393224 | tf_op jit(solution)/shard_map/ppermute | solution.py:18
  15.9 1.3 collective-permute-start.3
  17.2 10.7 %collective-permute-done.3.edges_ref = bf16[2,2,128,128]{3,2,1,0:T(8,128)(2,1)S(1)} collective-permute-done((bf16[2,2,128,128]{3,2,1,0:T(8,128)(2,1)S(1)}, bf16[2,2,128,128]{3,2,1,0:T(8,128)(2,1)S(1)}, u32[]{:S(2)}, u32[]{:S(2)}) %collective-permute-start.3) | collective-permute-done | bytes 131104 | tf_op jit(solution)/shard_map/ppermute | solution.py:18
  29.4 9.1 %wsum.3 = f32[3456,128]{1,0:T(8,128)} custom-call(bf16[4,8,128,128]{3,2,1,0:T(8,128)(2,1)} %grad_ref.3, bf16[4,1,128,128]{3,2,1,0:T(8,128)(2,1)} %copy-done.3, bf16[4,1,128,128]{3,2,1,0:T(8,128)(2,1)} %copy-done.2, bf16[2,8,128,128]{3,2,1,0:T(8,128)(2,1)} %copy-done.5, bf16[2,2,128,128]{3,2,1,0:T(8,128)(2,1)} %copy-done.7, bf16[4,8,128,128]{3,2,1,0:T(8,128)(2,1)} %saved_ref.7), custom_call_target="tpu_custom_call" | custom-call | flops 3623878656 | bytes 2097152 | tf_op jit(solution)/shard_map/wsum/pallas_call | solution.py:142
  38.5 1.5 reshape.13
  40.0 2.3 %copy.9 = f32[8,4,108,128]{3,0,2,1:T(8,128)} copy(f32[8,4,108,128]{3,2,1,0:T(8,128)S(1)} %reshape.13) | data formatting | bytes 3538944 | tf_op jit(solution)/shard_map/reshape | solution.py:171
  42.3 11.1 %spread.2.grad_ref = bf16[4,8,128,128]{3,2,1,0:T(8,128)(2,1)} custom-call(bf16[4,8,128,128]{3,2,1,0:T(8,128)(2,1)} %grad_ref.3, bf16[4,1,128,128]{3,2,1,0:T(8,128)(2,1)} %copy-done.3, bf16[4,1,128,128]{3,2,1,0:T(8,128)(2,1)} %copy-done.2, bf16[2,8,128,128]{3,2,1,0:T(8,128)(2,1)} %copy-done.5, bf16[2,2,128,128]{3,2,1,0:T(8,128)(2,1)} %copy-done.7, ...), custom_call_target="tpu_custom_call" | custom-call | flops 4831838208 | bytes 2097152 | tf_op jit(solution)/shard_map/spread/pallas_call | solution.py:124
  54.5 1.3 collective-permute-start.6
  56.8 1.3 collective-permute-start.5
  58.1 3.2 %collective-permute-start.4 = (bf16[4,1,128,128]{3,2,1,0:T(8,128)(2,1)S(1)}, bf16[4,1,128,128]{3,2,1,0:T(8,128)(2,1)S(1)}, u32[]{:S(2)}, u32[]{:S(2)}) collective-permute-start(bf16[4,1,128,128]{3,2,1,0:T(8,128)(2,1)S(1)} %get-tuple-element.4), channel_id=1, source_target_pairs={{0,1},{1,2},{2,3},{4,5},{5,6},{6,7},{8,9},{9,10},{10,11},{12,13},{... | collective-permute-start | bytes 393224 | tf_op jit(solution)/shard_map/ppermute | solution.py:18
  62.1 1.3 collective-permute-start.7
  63.4 9.0 %collective-permute-done.7.edges_ref = bf16[2,2,128,128]{3,2,1,0:T(8,128)(2,1)S(1)} collective-permute-done((bf16[2,2,128,128]{3,2,1,0:T(8,128)(2,1)S(1)}, bf16[2,2,128,128]{3,2,1,0:T(8,128)(2,1)S(1)}, u32[]{:S(2)}, u32[]{:S(2)}) %collective-permute-start.7) | collective-permute-done | bytes 131104 | tf_op jit(solution)/shard_map/ppermute | solution.py:18
  73.8 9.1 %wsum.2 = f32[3456,128]{1,0:T(8,128)} custom-call(bf16[4,8,128,128]{3,2,1,0:T(8,128)(2,1)} %spread.2.grad_ref, bf16[4,1,128,128]{3,2,1,0:T(8,128)(2,1)} %copy-done.1, bf16[4,1,128,128]{3,2,1,0:T(8,128)(2,1)} %copy-done, bf16[2,8,128,128]{3,2,1,0:T(8,128)(2,1)} %copy-done.4, bf16[2,2,128,128]{3,2,1,0:T(8,128)(2,1)} %copy-done.6, ...), custom_call_target="tpu_custom_call" | custom-call | flops 3623878656 | bytes 2097152 | tf_op jit(solution)/shard_map/wsum/pallas_call | solution.py:142
  82.9 1.5 reshape.12
  85.4 28.6 %all_to_all.10 = f32[8,4,108,128]{3,0,2,1:T(8,128)S(1)} all-to-all(f32[8,4,108,128]{3,0,2,1:T(8,128)S(1)} %copy.8), channel_id=1, replica_groups=mesh['tm'=8,'rows'=4] {'rows'}, dimensions={1} | all-to-all | bytes 3538944 | tf_op jit(solution)/shard_map/all_to_all | solution.py:158
  115.3 1.6 copy.10
  116.9 6.8 %all-to-all-start.1 = ((f32[8,2,108,128]{3,1,2,0:T(2,128)}), f32[8,2,108,128]{3,1,2,0:T(2,128)S(1)}, u32[]{:S(2)}, u32[]{:S(2)}) async-start(f32[8,2,108,128]{3,1,2,0:T(2,128)} %copy.10), calls=%async_computation.2 | async-start | bytes 1769472 | tf_op jit(solution)/shard_map/all_to_all | solution.py:158
  123.6 11.1 %spread.3 = bf16[4,8,128,128]{3,2,1,0:T(8,128)(2,1)} custom-call(bf16[4,8,128,128]{3,2,1,0:T(8,128)(2,1)} %spread.2.grad_ref, bf16[4,1,128,128]{3,2,1,0:T(8,128)(2,1)} %copy-done.1, bf16[4,1,128,128]{3,2,1,0:T(8,128)(2,1)} %copy-done, bf16[2,8,128,128]{3,2,1,0:T(8,128)(2,1)} %copy-done.4, bf16[2,2,128,128]{3,2,1,0:T(8,128)(2,1)} %copy-done.6, ...), custom_call_target="tpu_custom_call" | custom-call | flops 4831838208 | bytes 2097152 | tf_op jit(solution)/shard_map/spread/pallas_call | solution.py:124
  134.8 11.2 %all-to-all-done.1 = f32[8,2,108,128]{3,1,2,0:T(2,128)S(1)} async-done(((f32[8,2,108,128]{3,1,2,0:T(2,128)}), f32[8,2,108,128]{3,1,2,0:T(2,128)S(1)}, u32[]{:S(2)}, u32[]{:S(2)}) %all-to-all-start.1) | async-done | bytes 884768 | tf_op jit(solution)/shard_map/all_to_all | solution.py:158
  146.3 6.3 %all_gather.3 = f32[2,432,128]{2,0,1:T(2,128)S(1)} all-gather(f32[2,108,128]{2,0,1:T(2,128)S(1)} %broadcast_multiply_fusion), channel_id=1, replica_groups=mesh['tm'=8,'rows'=4] {'rows'}, dimensions={1}, use_global_device_ids=true | all-gather | bytes 552960 | tf_op jit(solution)/shard_map/all_gather | solution.py:174
  152.6 1.1 fusion.2
  (39 shorter events, 10.4 us)
Async XLA Ops:
  7.2 107.0 %reduce-scatter.2.cloned.1.call-start = ((), (), s32[]{:S(2)}) async-start(), calls=%async_computation.3 | async-start | bytes 2211840 | tf_op jit(solution)/shard_map/reduce_scatter | solution.py:171
  8.3 19.6 %collective-permute-start.2 = (bf16[2,8,128,128]{3,2,1,0:T(8,128)(2,1)S(1)}, bf16[2,8,128,128]{3,2,1,0:T(8,128)(2,1)S(1)}, u32[]{:S(2)}, u32[]{:S(2)}) collective-permute-start(bf16[2,8,128,128]{3,2,1,0:T(8,128)(2,1)S(1)} %slice.38), channel_id=1, source_target_pairs={{4,0},{8,4},{12,8},{16,12},{20,16},{24,20},{28,24},{5,1},{9,5},{13... | collective-permute-start | bytes 1572872 | tf_op jit(solution)/shard_map/ppermute | solution.py:18
  10.6 4.3 %collective-permute-start.1 = (bf16[4,1,128,128]{3,2,1,0:T(8,128)(2,1)S(1)}, bf16[4,1,128,128]{3,2,1,0:T(8,128)(2,1)S(1)}, u32[]{:S(2)}, u32[]{:S(2)}) collective-permute-start(bf16[4,1,128,128]{3,2,1,0:T(8,128)(2,1)S(1)} %get-tuple-element.5), channel_id=1, source_target_pairs={{1,0},{2,1},{3,2},{5,4},{6,5},{7,6},{9,8},{10,9},{11,10},{13,12},{... | collective-permute-start | bytes 393224 | tf_op jit(solution)/shard_map/ppermute | solution.py:18
  11.9 4.0 %collective-permute-start = (bf16[4,1,128,128]{3,2,1,0:T(8,128)(2,1)S(1)}, bf16[4,1,128,128]{3,2,1,0:T(8,128)(2,1)S(1)}, u32[]{:S(2)}, u32[]{:S(2)}) collective-permute-start(bf16[4,1,128,128]{3,2,1,0:T(8,128)(2,1)S(1)} %get-tuple-element.6), channel_id=1, source_target_pairs={{0,1},{1,2},{2,3},{4,5},{5,6},{6,7},{8,9},{9,10},{10,11},{12,13},{... | collective-permute-start | bytes 393224 | tf_op jit(solution)/shard_map/ppermute | solution.py:18
  14.9 13.0 %copy-start.2 = (bf16[4,1,128,128]{3,2,1,0:T(8,128)(2,1)}, bf16[4,1,128,128]{3,2,1,0:T(8,128)(2,1)S(1)}, u32[]{:S(2)}) copy-start(bf16[4,1,128,128]{3,2,1,0:T(8,128)(2,1)S(1)} %collective-permute-done.1.below_ref) | copy-start | bytes 393220
  15.9 12.0 %copy-start.3 = (bf16[4,1,128,128]{3,2,1,0:T(8,128)(2,1)}, bf16[4,1,128,128]{3,2,1,0:T(8,128)(2,1)S(1)}, u32[]{:S(2)}) copy-start(bf16[4,1,128,128]{3,2,1,0:T(8,128)(2,1)S(1)} %collective-permute-done.above_ref) | copy-start | bytes 393220
  15.9 12.0 %collective-permute-start.3 = (bf16[2,2,128,128]{3,2,1,0:T(8,128)(2,1)S(1)}, bf16[2,2,128,128]{3,2,1,0:T(8,128)(2,1)S(1)}, u32[]{:S(2)}, u32[]{:S(2)}) collective-permute-start(bf16[2,2,128,128]{3,2,1,0:T(8,128)(2,1)S(1)} %pad_maximum_fusion.1), channel_id=1, source_target_pairs={{4,0},{8,4},{12,8},{16,12},{20,16},{24,20},{28,24},{5,1},{9,5},{13... | collective-permute-start | bytes 393224 | tf_op jit(solution)/shard_map/ppermute | solution.py:18
  27.9 0.7 copy-start.7
  28.6 0.8 copy-start.5
  54.5 17.9 %collective-permute-start.6 = (bf16[2,8,128,128]{3,2,1,0:T(8,128)(2,1)S(1)}, bf16[2,8,128,128]{3,2,1,0:T(8,128)(2,1)S(1)}, u32[]{:S(2)}, u32[]{:S(2)}) collective-permute-start(bf16[2,8,128,128]{3,2,1,0:T(8,128)(2,1)S(1)} %slice.52), channel_id=1, source_target_pairs={{4,0},{8,4},{12,8},{16,12},{20,16},{24,20},{28,24},{5,1},{9,5},{13... | collective-permute-start | bytes 1572872 | tf_op jit(solution)/shard_map/ppermute | solution.py:18
  56.8 4.5 %collective-permute-start.5 = (bf16[4,1,128,128]{3,2,1,0:T(8,128)(2,1)S(1)}, bf16[4,1,128,128]{3,2,1,0:T(8,128)(2,1)S(1)}, u32[]{:S(2)}, u32[]{:S(2)}) collective-permute-start(bf16[4,1,128,128]{3,2,1,0:T(8,128)(2,1)S(1)} %get-tuple-element.3), channel_id=1, source_target_pairs={{1,0},{2,1},{3,2},{5,4},{6,5},{7,6},{9,8},{10,9},{11,10},{13,12},{... | collective-permute-start | bytes 393224 | tf_op jit(solution)/shard_map/ppermute | solution.py:18
  58.1 4.0 %collective-permute-start.4 = (bf16[4,1,128,128]{3,2,1,0:T(8,128)(2,1)S(1)}, bf16[4,1,128,128]{3,2,1,0:T(8,128)(2,1)S(1)}, u32[]{:S(2)}, u32[]{:S(2)}) collective-permute-start(bf16[4,1,128,128]{3,2,1,0:T(8,128)(2,1)S(1)} %get-tuple-element.4), channel_id=1, source_target_pairs={{0,1},{1,2},{2,3},{4,5},{5,6},{6,7},{8,9},{9,10},{10,11},{12,13},{... | collective-permute-start | bytes 393224 | tf_op jit(solution)/shard_map/ppermute | solution.py:18
  61.3 11.1 %copy-start = (bf16[4,1,128,128]{3,2,1,0:T(8,128)(2,1)}, bf16[4,1,128,128]{3,2,1,0:T(8,128)(2,1)S(1)}, u32[]{:S(2)}) copy-start(bf16[4,1,128,128]{3,2,1,0:T(8,128)(2,1)S(1)} %collective-permute-done.5.below_ref) | copy-start | bytes 393220
  62.1 10.3 %copy-start.1 = (bf16[4,1,128,128]{3,2,1,0:T(8,128)(2,1)}, bf16[4,1,128,128]{3,2,1,0:T(8,128)(2,1)S(1)}, u32[]{:S(2)}) copy-start(bf16[4,1,128,128]{3,2,1,0:T(8,128)(2,1)S(1)} %collective-permute-done.4.above_ref) | copy-start | bytes 393220
  62.1 10.3 %collective-permute-start.7 = (bf16[2,2,128,128]{3,2,1,0:T(8,128)(2,1)S(1)}, bf16[2,2,128,128]{3,2,1,0:T(8,128)(2,1)S(1)}, u32[]{:S(2)}, u32[]{:S(2)}) collective-permute-start(bf16[2,2,128,128]{3,2,1,0:T(8,128)(2,1)S(1)} %pad_maximum_fusion.2), channel_id=1, source_target_pairs={{4,0},{8,4},{12,8},{16,12},{20,16},{24,20},{28,24},{5,1},{9,5},{13... | collective-permute-start | bytes 393224 | tf_op jit(solution)/shard_map/ppermute | solution.py:18
  72.4 0.7 copy-start.6
  73.0 0.8 copy-start.4
  116.9 29.1 %all-to-all-start.1 = ((f32[8,2,108,128]{3,1,2,0:T(2,128)}), f32[8,2,108,128]{3,1,2,0:T(2,128)S(1)}, u32[]{:S(2)}, u32[]{:S(2)}) async-start(f32[8,2,108,128]{3,1,2,0:T(2,128)} %copy.10), calls=%async_computation.2 | async-start | bytes 1769472 | tf_op jit(solution)/shard_map/all_to_all | solution.py:158
Sparse Core Ops, SparseCore 0:
  42.4 31.5 reduce-scatter.1
where the time goes:
time: 161 us
  Pallas kernels  40.5 us (25%)
  blocking collectives  34.9 us (22%)
  waiting for transfers between devices  32.6 us (20%)
  starting transfers between devices  20.8 us (13%)
  local copies, waits for them, and re-layouts  16 us (10%)
  between operations  14.2 us (9%)
  other arithmetic  1.62 us (1%)
    all_to_all x1, blocking collectives, exchanged_sum(): lax.all_to_all(parts, axis, split_axis=dim, concat_axis=dim, tiled=True)  28.6 us
    pallas_call x2, Pallas kernels, spread_of(): pl.pallas_call(spread_kernel, out_shape=jax.ShapeDtypeStruct(saved.shape,...  22.3 us
    ppermute x8, waiting for transfers between devices, shifted(): return lax.ppermute(block, axis, route)  21.3 us
    pallas_call x2, Pallas kernels, wsum_of(): pl.pallas_call(wsum_kernel, out_shape=jax.ShapeDtypeStruct((27 * chans, c...  18.2 us
    ppermute x8, starting transfers between devices, shifted(): return lax.ppermute(block, axis, route)  14 us
    all_to_all x1, waiting for transfers between devices, exchanged_sum(): lax.all_to_all(parts, axis, split_axis=dim, concat_axis=dim, tiled=True)  11.2 us
    all_to_all x1, starting transfers between devices, exchanged_sum(): lax.all_to_all(parts, axis, split_axis=dim, concat_axis=dim, tiled=True)  6.77 us
    all_gather x1, blocking collectives, reduced(): whole = lax.all_gather(mine, 'rows', axis=1, tiled=True)  6.28 us
  transfers between devices with their start and end apart: 10, of which 5 were waited for; matrix products, arithmetic and copies ran while one was open for 4% of the time, Pallas kernels for 20%

commit v1 on v0

v1 whole, which is shorter than its diff:
```python
import functools
import math

import jax
import jax.numpy as jnp
from jax import lax
from jax.experimental import pallas as pl
from jax.experimental.pallas import tpu as pltpu
from jax.sharding import PartitionSpec as P

F32, BF16 = jnp.float32, jnp.bfloat16
VMEM_LIMIT = 60 * 1024 * 1024
MESH = pl.DeviceIdType.MESH


def plan(slots, bands, depth):
    share = depth // slots
    wire, unit = (BF16, 16) if share % 16 == 0 else (F32, 8)
    lanes = bands // 2
    chunk = -(-share // (bands * unit)) * unit
    return share, wire, unit, lanes, chunk, lanes * chunk


def whole_kernel(
    slots, bands, factor,
    up_hbm, first_hbm, second_hbm, weight_first_hbm, weight_second_hbm,
    out_ref, grad_first_ref, grad_second_ref,
    up, saved, weights, mid, wide, above, below, later, later_above, later_below, kernels, active, total,
    core_out, core_in, cross_out, cross_in, slot_sum, slot_out, slot_in, band_out, band_in,
    load_sem, row_send, row_recv, late_send, late_recv, edge_send, edge_recv,
    core_send, core_recv, cross_send, cross_recv, slot_send, slot_recv, band_send, band_recv,
):
    frames, height, width, chans = up.shape
    depth = 27 * chans
    share, wire, unit, lanes, chunk, half_rows = plan(slots, bands, depth)
    t, r = lax.axis_index("tm"), lax.axis_index("rows")
    core, lane = lax.rem(r, 2), r // 2
    has_above, has_below = r > 0, r < bands - 1
    has_prev, has_later = t > 0, t < slots - 1

    def remote(src, dst, send, recv, where):
        return pltpu.make_async_remote_copy(
            src_ref=src, dst_ref=dst, send_sem=send, recv_sem=recv, device_id=where, device_id_type=MESH
        )

    loads = [
        pltpu.make_async_copy(src, dst, load_sem.at[i])
        for i, (src, dst) in enumerate((
            (up_hbm, up), (weight_second_hbm, weights.at[1]), (second_hbm, saved.at[1]),
            (first_hbm, saved.at[0]), (weight_first_hbm, weights.at[0]),
        ))
    ]
    for load in loads:
        load.start()
    barrier = pltpu.get_barrier_semaphore()
    for step in range(1, bands):
        pl.semaphore_signal(barrier, inc=1, device_id=(t, lax.rem(r + step, bands)), device_id_type=MESH)
    for step in range(1, slots):
        pl.semaphore_signal(barrier, inc=1, device_id=(lax.rem(t + step, slots), r), device_id_type=MESH)
    loads[0].wait()
    pl.semaphore_wait(barrier, bands + slots - 2)

    def row_up(layer, grad, low, count, index):
        part = pl.ds(low, count)
        return remote(grad.at[part, 0], below.at[layer, part], row_send.at[layer, index, 0], row_recv.at[layer, index, 0], (t, r - 1))

    def row_down(layer, grad, low, count, index):
        part = pl.ds(low, count)
        return remote(grad.at[part, height - 1], above.at[layer, part], row_send.at[layer, index, 1], row_recv.at[layer, index, 1], (t, r + 1))

    def late(layer, grad, frame):
        return remote(grad.at[frame], later.at[layer, frame], late_send.at[layer, frame], late_recv.at[layer, frame], (t - 1, r))

    def edge_up(layer, frame):
        return remote(later.at[layer, frame, 0], later_below.at[layer, frame], edge_send.at[layer, frame, 0], edge_recv.at[layer, frame, 0], (t, r - 1))

    def edge_down(layer, frame):
        return remote(later.at[layer, frame, height - 1], later_above.at[layer, frame], edge_send.at[layer, frame, 1], edge_recv.at[layer, frame, 1], (t, r + 1))

    def when(flag, *actions):
        @pl.when(flag)
        def _():
            for action in actions:
                action()

    def send_rows(layer, grad, low, count, index):
        when(has_above, lambda: row_up(layer, grad, low, count, index).start())
        when(has_below, lambda: row_down(layer, grad, low, count, index).start())

    def send_late(layer, grad):
        when(has_prev, *[lambda f=f: late(layer, grad, f).start() for f in range(2)])

    place = lax.broadcasted_iota(jnp.int32, (width, chans), 0)

    def fill_row(layer, value, frame, row):
        spread = value.astype(F32)
        after = jnp.where(place == width - 1, 0.0, pltpu.roll(spread, width - 1, 0)).astype(BF16)
        before = jnp.where(place == 0, 0.0, pltpu.roll(spread, 1, 0)).astype(BF16)
        lines = pl.ds(row * width, width) if isinstance(row, int) else pl.ds(pl.multiple_of(row * width, width), width)
        wide[layer, frame, lines, pl.ds(0, chans)] = after
        wide[layer, frame, lines, pl.ds(chans, chans)] = value
        wide[layer, frame, lines, pl.ds(2 * chans, chans)] = before

    def zero_row(layer, frame, row):
        wide[layer, frame, pl.ds(row * width, width), :] = jnp.zeros((width, 3 * chans), BF16)

    def fill_frames(layer, grad, low, high, base=0):
        def one(row, carry):
            for frame in range(low, high):
                fill_row(layer, grad[frame - base, row], frame, row + 1)
            return carry

        lax.fori_loop(0, height, one, 0)

    def take_rows(layer, grad, low, count, index):
        def got_above():
            row_down(layer, grad, low, count, index).wait_recv()
            for frame in range(low, low + count):
                fill_row(layer, above[layer, frame], frame, 0)

        def got_below():
            row_up(layer, grad, low, count, index).wait_recv()
            for frame in range(low, low + count):
                fill_row(layer, below[layer, frame], frame, height + 1)

        when(has_above, got_above)
        when(has_below, got_below)
        when(jnp.logical_not(has_above), *[lambda f=f: zero_row(layer, f, 0) for f in range(low, low + count)])
        when(jnp.logical_not(has_below), *[lambda f=f: zero_row(layer, f, height + 1) for f in range(low, low + count)])

    def take_late(layer, grad):
        def forward(frame):
            late(layer, grad, frame).wait_recv()
            when(has_above, lambda: edge_up(layer, frame).start())
            when(has_below, lambda: edge_down(layer, frame).start())
            fill_frames(layer, later.at[layer], frames + frame, frames + frame + 1, base=frames)

        def edges(frame):
            def got_above():
                edge_down(layer, frame).wait_recv()
                fill_row(layer, later_above[layer, frame], frames + frame, 0)

            def got_below():
                edge_up(layer, frame).wait_recv()
                fill_row(layer, later_below[layer, frame], frames + frame, height + 1)

            when(has_above, got_above)
            when(has_below, got_below)
            when(jnp.logical_not(has_above), lambda: zero_row(layer, frames + frame, 0))
            when(jnp.logical_not(has_below), lambda: zero_row(layer, frames + frame, height + 1))

        when(has_later, *[lambda f=f: forward(f) for f in range(2)], *[lambda f=f: edges(f) for f in range(2)])

        @pl.when(jnp.logical_not(has_later))
        def _():
            for frame in range(2):
                wide[layer, frames + frame] = jnp.zeros(wide.shape[2:], BF16)

    def make_kernels(layer):
        span = 9 * chans
        for half in range(2):
            for j in range(4):
                p = 2 + half - j
                for tap in range(9):
                    block = (
                        weights[layer, pl.ds((9 * p + tap) * chans, chans), :]
                        if 0 <= p < 3
                        else jnp.zeros((chans, chans), BF16)
                    )
                    kernels[layer, pl.ds(half * chans, chans), pl.ds(j * span + tap * chans, chans)] = block

    def make_active(layer):
        def one(frame, carry):
            for row in range(height):
                value = saved[layer, frame, row].astype(F32)
                act = value * jax.nn.sigmoid(value)
                lines = pl.ds(pl.multiple_of(frame * chans, chans), chans)
                active[layer, lines, pl.ds(row * width, width)] = act.T.astype(BF16)
            return carry

        lax.fori_loop(0, frames, one, 0)

    step_rows = math.gcd(4, height)
    lines = step_rows * width

    def spread(layer, pair, target):
        def one(index, carry):
            parts = [
                wide[layer, 2 * pair + j, pl.ds(pl.multiple_of(index * lines + (2 - q) * width, width), lines), :]
                for j in range(4)
                for q in range(3)
            ]
            sums = lax.dot_general(
                jnp.concatenate(parts, axis=1), kernels[layer], (((1,), (1,)), ((), ())), preferred_element_type=F32
            )
            for half in range(2):
                rows = pl.ds(index * step_rows, step_rows)
                value = saved[layer, 2 * pair + half, rows].reshape(lines, chans).astype(F32)
                sigma = jax.nn.sigmoid(value)
                slope = sigma * (1.0 + value * (1.0 - sigma))
                result = sums[:, half * chans : (half + 1) * chans] * slope
                target[2 * pair + half, rows] = result.astype(BF16).reshape(step_rows, width, chans)
            return carry

        lax.fori_loop(0, height // step_rows, one, 0)

    def wsum(layer, frame):
        low, high = max(0, frame - 2), min(frames, frame + 1)
        acts = active[layer, pl.ds(low * chans, (high - low) * chans), :]
        part = jnp.concatenate([wide[layer, frame, pl.ds((2 - q) * width, height * width), :] for q in range(3)], axis=1)
        sums = jnp.dot(acts, part, preferred_element_type=F32)
        for s in range(low, high):
            p = s + 2 - frame
            for tap in range(9):
                rows = pl.ds((9 * p + tap) * chans, chans)
                block = sums[(s - low) * chans : (s - low + 1) * chans, tap * chans : (tap + 1) * chans]
                total[layer, rows, :] = block if s == 0 else total[layer, rows, :] + block

    half_at = lambda which: which * (share - half_rows)
    aligned = lambda value: pl.multiple_of(value, unit)

    def core_copy(layer):
        return remote(core_out.at[layer], core_in.at[layer], core_send.at[layer], core_recv.at[layer], (t, 2 * lane + 1 - core))

    def reduce_core(layer):
        for slot in range(slots):
            lines = pl.ds(aligned(slot * share + half_at(1 - core)), half_rows)
            core_out[layer, slot] = total[layer, lines, :].astype(wire)
        core_copy(layer).start()

    def cross_copy(layer, step):
        to = lax.rem(lane + step, lanes)
        src = cross_out.at[layer, :, pl.ds(aligned(to * chunk), chunk)]
        return remote(src, cross_in.at[layer, step - 1], cross_send.at[layer, step - 1], cross_recv.at[layer, step - 1], (t, 2 * to + core))

    def reduce_cross(layer):
        core_copy(layer).wait_recv()
        for slot in range(slots):
            lines = pl.ds(aligned(slot * share + half_at(core)), half_rows)
            cross_out[layer, slot] = (total[layer, lines, :] + core_in[layer, slot].astype(F32)).astype(wire)
        for step in range(1, lanes):
            cross_copy(layer, step).start()

    def slot_copy(layer, step):
        to = lax.rem(t + step, slots)
        return remote(slot_out.at[layer, to], slot_in.at[layer, step - 1], slot_send.at[layer, step - 1], slot_recv.at[layer, step - 1], (to, r))

    def reduce_slots(layer):
        for step in range(1, lanes):
            cross_copy(layer, step).wait_recv()
        for slot in range(slots):
            lines = pl.ds(aligned(slot * share + half_at(core) + lane * chunk), chunk)
            mine = pl.ds(aligned(lane * chunk), chunk)
            value = total[layer, lines, :] + core_in[layer, slot, mine, :].astype(F32)
            for step in range(1, lanes):
                value = value + cross_in[layer, step - 1, slot].astype(F32)
            slot_sum[layer, slot] = value
            slot_out[layer, slot] = value.astype(wire)
        for step in range(1, slots):
            slot_copy(layer, step).start()

    def band_copy(layer, step):
        to = lax.rem(r + step, bands)
        return remote(band_out.at[layer], band_in.at[layer, step - 1], band_send.at[layer, step - 1], band_recv.at[layer, step - 1], (t, to))

    def reduce_bands(layer):
        for step in range(1, slots):
            slot_copy(layer, step).wait_recv()
        value = slot_sum[layer, t]
        for step in range(1, slots):
            value = value + slot_in[layer, step - 1].astype(F32)
        band_out[layer] = value * factor
        for step in range(1, bands):
            band_copy(layer, step).start()

    def band_lines(band):
        return pl.ds(aligned(half_at(lax.rem(band, 2)) + (band // 2) * chunk), chunk)

    def finish(layer, target):
        target[band_lines(r), :] = band_out[layer]
        for step in range(1, bands):
            band_copy(layer, step).wait_recv()
            target[band_lines(lax.rem(r - step + bands, bands)), :] = band_in[layer, step - 1]

    send_rows(1, up, 0, frames, 0)
    send_late(1, up)
    fill_frames(1, up, 0, frames)
    loads[1].wait()
    make_kernels(1)
    take_rows(1, up, 0, frames, 0)
    loads[2].wait()
    spread(1, 0, mid)
    send_late(0, mid)
    send_rows(0, mid, 0, 2, 0)
    make_active(1)
    for frame in range(frames):
        wsum(1, frame)
    loads[3].wait()
    loads[4].wait()
    make_kernels(0)
    make_active(0)
    fill_frames(0, mid, 0, 2)
    take_late(1, up)
    for pair in range(1, frames // 2):
        spread(1, pair, mid)
        send_rows(0, mid, 2 * pair, 2, pair)
    for frame in range(frames, frames + 2):
        wsum(1, frame)
    reduce_core(1)

    fill_frames(0, mid, 2, frames)
    for pair in range(frames // 2):
        take_rows(0, mid, 2 * pair, 2, pair)
    reduce_cross(1)
    for frame in range(frames):
        wsum(0, frame)
    reduce_slots(1)
    take_late(0, mid)
    for frame in range(frames, frames + 2):
        wsum(0, frame)
    reduce_core(0)
    reduce_bands(1)
    spread(0, 0, out_ref)
    reduce_cross(0)
    for pair in range(1, frames // 2):
        spread(0, pair, out_ref)
    finish(1, grad_second_ref)
    reduce_slots(0)
    reduce_bands(0)
    finish(0, grad_first_ref)

    def sent(*copies):
        for copy in copies:
            copy.wait_send()

    when(has_above, lambda: sent(row_up(1, up, 0, frames, 0), *[row_up(0, mid, 2 * p, 2, p) for p in range(frames // 2)]))
    when(has_below, lambda: sent(row_down(1, up, 0, frames, 0), *[row_down(0, mid, 2 * p, 2, p) for p in range(frames // 2)]))
    when(has_prev, lambda: sent(*[late(1, up, f) for f in range(2)], *[late(0, mid, f) for f in range(2)]))
    for flag, copy in ((has_above, edge_up), (has_below, edge_down)):
        when(jnp.logical_and(has_later, flag), lambda copy=copy: sent(*[copy(layer, f) for layer in range(2) for f in range(2)]))
    for layer in range(2):
        sent(core_copy(layer))
        sent(*[cross_copy(layer, step) for step in range(1, lanes)])
        sent(*[slot_copy(layer, step) for step in range(1, slots)])
        sent(*[band_copy(layer, step) for step in range(1, bands)])


def body(upstream, saved_first, saved_second, weight_first, weight_second):
    slots, bands = lax.axis_size("tm"), lax.axis_size("rows")
    frames, height, width, chans = upstream.shape
    depth = 27 * chans
    share, wire, unit, lanes, chunk, half_rows = plan(slots, bands, depth)
    factor = 1.0 / math.sqrt(frames * slots * height * bands * width)
    pairs = frames // 2
    vmem, dma = pltpu.VMEM, pltpu.SemaphoreType.DMA
    scratch = [
        vmem((frames, height, width, chans), BF16),
        vmem((2, frames, height, width, chans), BF16),
        vmem((2, depth, chans), BF16),
        vmem((frames, height, width, chans), BF16),
        vmem((2, frames + 2, (height + 2) * width, 3 * chans), BF16),
        vmem((2, frames, width, chans), BF16),
        vmem((2, frames, width, chans), BF16),
        vmem((2, 2, height, width, chans), BF16),
        vmem((2, 2, width, chans), BF16),
        vmem((2, 2, width, chans), BF16),
        vmem((2, 2 * chans, 36 * chans), BF16),
        vmem((2, frames * chans, height * width), BF16),
        vmem((2, depth, chans), F32),
        vmem((2, slots, half_rows, chans), wire),
        vmem((2, slots, half_rows, chans), wire),
        vmem((2, slots, half_rows, chans), wire),
        vmem((2, max(1, lanes - 1), slots, chunk, chans), wire),
        vmem((2, slots, chunk, chans), F32),
        vmem((2, slots, chunk, chans), wire),
        vmem((2, slots - 1, chunk, chans), wire),
        vmem((2, chunk, chans), F32),
        vmem((2, bands - 1, chunk, chans), F32),
        dma((5,)),
        dma((2, pairs, 2)), dma((2, pairs, 2)),
        dma((2, 2)), dma((2, 2)),
        dma((2, 2, 2)), dma((2, 2, 2)),
        dma((2,)), dma((2,)),
        dma((2, max(1, lanes - 1))), dma((2, max(1, lanes - 1))),
        dma((2, slots - 1)), dma((2, slots - 1)),
        dma((2, bands - 1)), dma((2, bands - 1)),
    ]
    return pl.pallas_call(
        functools.partial(whole_kernel, slots, bands, factor),
        out_shape=[
            jax.ShapeDtypeStruct(upstream.shape, BF16),
            jax.ShapeDtypeStruct((share, chans), F32),
            jax.ShapeDtypeStruct((share, chans), F32),
        ],
        in_specs=[pl.BlockSpec(memory_space=pl.ANY)] * 5,
        out_specs=[pl.BlockSpec(memory_space=pltpu.VMEM)] * 3,
        scratch_shapes=scratch,
        compiler_params=pltpu.CompilerParams(vmem_limit_bytes=VMEM_LIMIT, collective_id=0, has_side_effects=True),
        name="whole",
    )(upstream, saved_first, saved_second, weight_first, weight_second)


def solution(mesh):
    grid = P("tm", "rows", None, None)
    return jax.shard_map(
        body,
        mesh=mesh,
        in_specs=(grid, grid, grid, P(), P()),
        out_specs=(grid, P("tm", None), P("tm", None)),
        check_vma=False,
    )
```

time: 161 us -> 64.7 us (0.40)
  blocking collectives: 34.9 us -> 0 us
  waiting for transfers between devices: 32.6 us -> 0 us
  starting transfers between devices: 20.8 us -> 0 us
  Pallas kernels: 40.5 us -> 59.5 us
  between operations: 14.2 us -> 0.65 us
  local copies, waits for them, and re-layouts: 16 us -> 4.05 us
  other arithmetic: 1.62 us -> 0 us
    all_to_all x1 -> x0, blocking collectives: 28.6 us -> none  [exchanged_sum(): lax.all_to_all(parts, axis, split_axis=dim, concat_axis=dim, tiled=True)]
    ppermute x8 -> x0, waiting for transfers between devices: 21.3 us -> none  [shifted(): return lax.ppermute(block, axis, route)]
    pallas_call x4 -> x1, Pallas kernels: 40.5 us -> 59.5 us  [body(): pl.pallas_call(functools.partial(whole_kernel, slots, bands, factor), out...]
    ppermute x8 -> x0, starting transfers between devices: 14 us -> none  [shifted(): return lax.ppermute(block, axis, route)]
    all_to_all x1 -> x0, waiting for transfers between devices: 11.2 us -> none  [exchanged_sum(): lax.all_to_all(parts, axis, split_axis=dim, concat_axis=dim, tiled=True)]
    all_to_all x1 -> x0, starting transfers between devices: 6.77 us -> none  [exchanged_sum(): lax.all_to_all(parts, axis, split_axis=dim, concat_axis=dim, tiled=True)]
    all_gather x1 -> x0, blocking collectives: 6.28 us -> none  [reduced(): whole = lax.all_gather(mine, 'rows', axis=1, tiled=True)]
    reshape x4 -> x0, local copies, waits for them, and re-layouts: 6.26 us -> none  [the longest x2 3.75 us: reduced(): wsum_second.reshape(split)]
  transfers between devices with their start and end apart: 10 -> 0, of which waited for: 5 -> 0; matrix products, arithmetic and copies ran while one was open for 4% -> 0% of each run, Pallas kernels for 20% -> 0%
where the time goes in v1:
time: 64.7 us; the launch traced here: 64.2 us
  Pallas kernels  59.5 us (92%)
  local copies, waits for them, and re-layouts  4.05 us (6%)
  between operations  0.65 us (1%)
    pallas_call x1, Pallas kernels, body(): pl.pallas_call(functools.partial(whole_kernel, slots, bands, factor), out...  59.5 us
    unnamed x7, local copies, waits for them, and re-layouts  4.05 us

profile of v1, /device:TPU:0, one launch (start us, length us, event | category | flops | bytes accessed | tf_op | source)
XLA Modules:
  0.0 64.2 jit_solution(2746002222638051621)
XLA Ops:
  0.6 59.5 %whole.1 = (bf16[4,8,128,128]{3,2,1,0:T(8,128)(2,1)}, f32[432,128]{1,0:T(8,128)}, f32[432,128]{1,0:T(8,128)}) custom-call(bf16[4,8,128,128]{3,2,1,0:T(8,128)(2,1)} %up_hbm.1, bf16[4,8,128,128]{3,2,1,0:T(8,128)(2,1)} %first_hbm.1, bf16[4,8,128,128]{3,2,1,0:T(8,128)(2,1)} %second_hbm.1, bf16[3456,128]{1,0:T(8,128)(2,1)} %weight_first_hbm.1, ...), custom_call_target="tpu_custom_call" | custom-call | tf_op jit(solution)/shard_map/whole/pallas_call | solution.py:388
  60.2 0.0 copy-start.1
  60.2 2.3 %copy.11 = bf16[4,8,128,128]{3,2,1,0:T(8,128)(2,1)} copy(bf16[4,8,128,128]{3,2,1,0:T(8,128)(2,1)} %get-tuple-element.6) | data formatting | bytes 2097152
  62.5 0.0 copy-done.1
  62.5 0.0 copy-start
  62.5 0.7 %copy.12 = f32[432,128]{1,0:T(8,128)} copy(f32[432,128]{1,0:T(8,128)S(1)} %copy-done.1) | data formatting | bytes 442368
  63.2 0.3 copy-done
  63.5 0.7 %copy.13 = f32[432,128]{1,0:T(8,128)} copy(f32[432,128]{1,0:T(8,128)S(1)} %copy-done) | data formatting | bytes 442368
Async XLA Ops:
  60.2 2.4 %copy-start.1 = (f32[432,128]{1,0:T(8,128)S(1)}, f32[432,128]{1,0:T(8,128)}, u32[]{:S(2)}) copy-start(f32[432,128]{1,0:T(8,128)} %get-tuple-element.7) | copy-start | bytes 663556
  62.5 1.0 %copy-start = (f32[432,128]{1,0:T(8,128)S(1)}, f32[432,128]{1,0:T(8,128)}, u32[]{:S(2)}) copy-start(f32[432,128]{1,0:T(8,128)} %get-tuple-element.8) | copy-start | bytes 663556

commit v2 on v1

--- a/solution.py
+++ b/solution.py
@@ -9,7 +9,7 @@
 from jax.sharding import PartitionSpec as P
 
 F32, BF16 = jnp.float32, jnp.bfloat16
-VMEM_LIMIT = 60 * 1024 * 1024
+VMEM_LIMIT = 52 * 1024 * 1024
 MESH = pl.DeviceIdType.MESH
 
 
@@ -26,7 +26,7 @@
     up_hbm, first_hbm, second_hbm, weight_first_hbm, weight_second_hbm,
     out_ref, grad_first_ref, grad_second_ref,
     up, saved, weights, mid, wide, above, below, later, later_above, later_below, kernels, active, total,
-    core_out, core_in, cross_out, cross_in, slot_sum, slot_out, slot_in, band_out, band_in,
+    core_out, core_in, cross_out, cross_in, slot_sum, slot_out, slot_in, band_in,
     load_sem, row_send, row_recv, late_send, late_recv, edge_send, edge_recv,
     core_send, core_recv, cross_send, cross_recv, slot_send, slot_recv, band_send, band_recv,
 ):
@@ -128,13 +128,21 @@
         when(jnp.logical_not(has_above), *[lambda f=f: zero_row(layer, f, 0) for f in range(low, low + count)])
         when(jnp.logical_not(has_below), *[lambda f=f: zero_row(layer, f, height + 1) for f in range(low, low + count)])
 
-    def take_late(layer, grad):
+    def forward_late(layer, grad):
         def forward(frame):
             late(layer, grad, frame).wait_recv()
             when(has_above, lambda: edge_up(layer, frame).start())
             when(has_below, lambda: edge_down(layer, frame).start())
             fill_frames(layer, later.at[layer], frames + frame, frames + frame + 1, base=frames)
 
+        when(has_later, *[lambda f=f: forward(f) for f in range(2)])
+
+        @pl.when(jnp.logical_not(has_later))
+        def _():
+            for frame in range(2):
+                wide[layer, frames + frame] = jnp.zeros(wide.shape[2:], BF16)
+
+    def take_edges(layer):
         def edges(frame):
             def got_above():
                 edge_down(layer, frame).wait_recv()
@@ -149,12 +157,7 @@
             when(jnp.logical_not(has_above), lambda: zero_row(layer, frames + frame, 0))
             when(jnp.logical_not(has_below), lambda: zero_row(layer, frames + frame, height + 1))
 
-        when(has_later, *[lambda f=f: forward(f) for f in range(2)], *[lambda f=f: edges(f) for f in range(2)])
-
-        @pl.when(jnp.logical_not(has_later))
-        def _():
-            for frame in range(2):
-                wide[layer, frames + frame] = jnp.zeros(wide.shape[2:], BF16)
+        when(has_later, *[lambda f=f: edges(f) for f in range(2)])
 
     def make_kernels(layer):
         span = 9 * chans
@@ -183,15 +186,15 @@
     step_rows = math.gcd(4, height)
     lines = step_rows * width
 
-    def spread(layer, pair, target):
+    def spread(layer, pair, target, low=0, high=height // step_rows):
         def one(index, carry):
-            parts = [
+            pieces = [
                 wide[layer, 2 * pair + j, pl.ds(pl.multiple_of(index * lines + (2 - q) * width, width), lines), :]
                 for j in range(4)
                 for q in range(3)
             ]
             sums = lax.dot_general(
-                jnp.concatenate(parts, axis=1), kernels[layer], (((1,), (1,)), ((), ())), preferred_element_type=F32
+                jnp.concatenate(pieces, axis=1), kernels[layer], (((1,), (1,)), ((), ())), preferred_element_type=F32
             )
             for half in range(2):
                 rows = pl.ds(index * step_rows, step_rows)
@@ -202,132 +205,191 @@
                 target[2 * pair + half, rows] = result.astype(BF16).reshape(step_rows, width, chans)
             return carry
 
-        lax.fori_loop(0, height // step_rows, one, 0)
-
-    def wsum(layer, frame):
+        lax.fori_loop(low, high, one, 0)
+
+    def wsum(layer, frame, taps=(0, 1, 2)):
         low, high = max(0, frame - 2), min(frames, frame + 1)
         acts = active[layer, pl.ds(low * chans, (high - low) * chans), :]
-        part = jnp.concatenate([wide[layer, frame, pl.ds((2 - q) * width, height * width), :] for q in range(3)], axis=1)
+        part = jnp.concatenate([wide[layer, frame, pl.ds((2 - q) * width, height * width), :] for q in taps], axis=1)
         sums = jnp.dot(acts, part, preferred_element_type=F32)
         for s in range(low, high):
             p = s + 2 - frame
-            for tap in range(9):
+            for i, tap in enumerate(3 * q + k for q in taps for k in range(3)):
                 rows = pl.ds((9 * p + tap) * chans, chans)
-                block = sums[(s - low) * chans : (s - low + 1) * chans, tap * chans : (tap + 1) * chans]
+                block = sums[(s - low) * chans : (s - low + 1) * chans, i * chans : (i + 1) * chans]
                 total[layer, rows, :] = block if s == 0 else total[layer, rows, :] + block
 
     half_at = lambda which: which * (share - half_rows)
     aligned = lambda value: pl.multiple_of(value, unit)
-
-    def core_copy(layer):
-        return remote(core_out.at[layer], core_in.at[layer], core_send.at[layer], core_recv.at[layer], (t, 2 * lane + 1 - core))
-
-    def reduce_core(layer):
-        for slot in range(slots):
+    settled = min(slots, -(-18 * chans // share))
+    groups = [(low, high) for low, high in ((0, settled), (settled, slots)) if low < high]
+    first_rows = -(-chunk // (2 * unit)) * unit
+    parts = [(low, count) for low, count in ((0, first_rows), (first_rows, chunk - first_rows)) if count > 0]
+    own_half = lambda slot: aligned(slot * share + half_at(core))
+
+    def core_copy(layer, group):
+        low, high = groups[group]
+        range_ = pl.ds(low, high - low)
+        return remote(
+            core_out.at[layer, range_], core_in.at[layer, range_],
+            core_send.at[layer, group], core_recv.at[layer, group], (t, 2 * lane + 1 - core),
+        )
+
+    def reduce_core(layer, group):
+        for slot in range(*groups[group]):
             lines = pl.ds(aligned(slot * share + half_at(1 - core)), half_rows)
             core_out[layer, slot] = total[layer, lines, :].astype(wire)
-        core_copy(layer).start()
-
-    def cross_copy(layer, step):
+        core_copy(layer, group).start()
+
+    def cross_copy(layer, group, part, step):
+        low, high = groups[group]
+        line, count = parts[part]
         to = lax.rem(lane + step, lanes)
-        src = cross_out.at[layer, :, pl.ds(aligned(to * chunk), chunk)]
-        return remote(src, cross_in.at[layer, step - 1], cross_send.at[layer, step - 1], cross_recv.at[layer, step - 1], (t, 2 * to + core))
-
-    def reduce_cross(layer):
-        core_copy(layer).wait_recv()
+        return remote(
+            cross_out.at[layer, pl.ds(low, high - low), pl.ds(aligned(to * chunk + line), count)],
+            cross_in.at[layer, step - 1, pl.ds(low, high - low), pl.ds(line, count)],
+            cross_send.at[layer, group, part, step - 1], cross_recv.at[layer, group, part, step - 1], (t, 2 * to + core),
+        )
+
+    def reduce_cross(layer, group):
+        core_copy(layer, group).wait_recv()
+        for slot in range(*groups[group]):
+            cross_out[layer, slot] = (
+                total[layer, pl.ds(own_half(slot), half_rows), :] + core_in[layer, slot].astype(F32)
+            ).astype(wire)
+        for part in range(len(parts)):
+            for step in range(1, lanes):
+                cross_copy(layer, group, part, step).start()
+
+    def slot_copy(layer, part, step):
+        to = lax.rem(t + step, slots)
+        lines = pl.ds(*parts[part])
+        return remote(
+            slot_out.at[layer, to, lines], slot_in.at[layer, step - 1, lines],
+            slot_send.at[layer, part, step - 1], slot_recv.at[layer, part, step - 1], (to, r),
+        )
+
+    def reduce_slots(layer, part):
+        line, count = parts[part]
+        for group in range(len(groups)):
+            for step in range(1, lanes):
+                cross_copy(layer, group, part, step).wait_recv()
         for slot in range(slots):
-            lines = pl.ds(aligned(slot * share + half_at(core)), half_rows)
-            cross_out[layer, slot] = (total[layer, lines, :] + core_in[layer, slot].astype(F32)).astype(wire)
-        for step in range(1, lanes):
-            cross_copy(layer, step).start()
-
-    def slot_copy(layer, step):
-        to = lax.rem(t + step, slots)
-        return remote(slot_out.at[layer, to], slot_in.at[layer, step - 1], slot_send.at[layer, step - 1], slot_recv.at[layer, step - 1], (to, r))
-
-    def reduce_slots(layer):
-        for step in range(1, lanes):
-            cross_copy(layer, step).wait_recv()
-        for slot in range(slots):
-            lines = pl.ds(aligned(slot * share + half_at(core) + lane * chunk), chunk)
-            mine = pl.ds(aligned(lane * chunk), chunk)
-            value = total[layer, lines, :] + core_in[layer, slot, mine, :].astype(F32)
+            mine = aligned(lane * chunk + line)
+            value = total[layer, pl.ds(aligned(own_half(slot) + mine), count), :]
+            value = value + core_in[layer, slot, pl.ds(mine, count), :].astype(F32)
             for step in range(1, lanes):
-                value = value + cross_in[layer, step - 1, slot].astype(F32)
-            slot_sum[layer, slot] = value
-            slot_out[layer, slot] = value.astype(wire)
+                value = value + cross_in[layer, step - 1, slot, pl.ds(line, count), :].astype(F32)
+            slot_sum[layer, slot, pl.ds(line, count), :] = value
+            slot_out[layer, slot, pl.ds(line, count), :] = value.astype(wire)
         for step in range(1, slots):
-            slot_copy(layer, step).start()
-
-    def band_copy(layer, step):
+            slot_copy(layer, part, step).start()
+
+    def band_copy(layer, part, step):
         to = lax.rem(r + step, bands)
-        return remote(band_out.at[layer], band_in.at[layer, step - 1], band_send.at[layer, step - 1], band_recv.at[layer, step - 1], (t, to))
-
-    def reduce_bands(layer):
+        lines = pl.ds(*parts[part])
+        return remote(
+            band_in.at[layer, 0, lines], band_in.at[layer, step, lines],
+            band_send.at[layer, part, step - 1], band_recv.at[layer, part, step - 1], (t, to),
+        )
+
+    def reduce_bands(layer, part):
+        lines = pl.ds(*parts[part])
         for step in range(1, slots):
-            slot_copy(layer, step).wait_recv()
-        value = slot_sum[layer, t]
+            slot_copy(layer, part, step).wait_recv()
+        value = slot_sum[layer, t, lines, :]
         for step in range(1, slots):
-            value = value + slot_in[layer, step - 1].astype(F32)
-        band_out[layer] = value * factor
+            value = value + slot_in[layer, step - 1, lines, :].astype(F32)
+        band_in[layer, 0, lines, :] = (value * factor).astype(wire)
         for step in range(1, bands):
-            band_copy(layer, step).start()
-
-    def band_lines(band):
-        return pl.ds(aligned(half_at(lax.rem(band, 2)) + (band // 2) * chunk), chunk)
+            band_copy(layer, part, step).start()
 
     def finish(layer, target):
-        target[band_lines(r), :] = band_out[layer]
-        for step in range(1, bands):
-            band_copy(layer, step).wait_recv()
-            target[band_lines(lax.rem(r - step + bands, bands)), :] = band_in[layer, step - 1]
+        for part in range(len(parts)):
+            for step in range(1, bands):
+                band_copy(layer, part, step).wait_recv()
+        for band in range(bands):
+            lines = pl.ds((band % 2) * (share - half_rows) + (band // 2) * chunk, chunk)
+            target[lines, :] = band_in[layer, lax.rem(r - band + bands, bands)].astype(F32)
+
+    def run(name, action, *args):
+        with jax.named_scope(name):
+            action(*args)
+
+    chunks = height // step_rows
+    late_frames = range(frames, frames + 2)
+
+    zero = r // bands
 
     send_rows(1, up, 0, frames, 0)
     send_late(1, up)
-    fill_frames(1, up, 0, frames)
+    run("fill", fill_frames, 1, up, 0, frames)
     loads[1].wait()
-    make_kernels(1)
-    take_rows(1, up, 0, frames, 0)
+    run("kernels", make_kernels, 1)
     loads[2].wait()
-    spread(1, 0, mid)
+    run("active", make_active, 1)
+    loads[3].wait()
+    run("active", make_active, 0)
+    loads[4].wait()
+    run("kernels", make_kernels, 0)
+    run("take_rows", take_rows, 1, up, 0, frames, 0)
+    run("spread", spread, 1, 0, mid)
+    send_rows(0, mid, 0, 2, 0)
     send_late(0, mid)
-    send_rows(0, mid, 0, 2, 0)
-    make_active(1)
-    for frame in range(frames):
-        wsum(1, frame)
-    loads[3].wait()
-    loads[4].wait()
-    make_kernels(0)
-    make_active(0)
-    fill_frames(0, mid, 0, 2)
-    take_late(1, up)
+    run("fill", fill_frames, 0, mid, 0, 2)
+    for frame in range(frames - 1):
+        run("wsum", wsum, 1, frame)
+    run("take_rows", take_rows, 0, mid, 0, 2, 0)
+    for frame in range(2):
+        run("wsum", wsum, 0, frame)
+    run("fwd_late", forward_late, 1, up)
+    run("wsum", wsum, 1, frames - 1)
+    for frame in late_frames:
+        run("wsum", wsum, 1, frame, (1,))
+    run("edges", take_edges, 1)
     for pair in range(1, frames // 2):
-        spread(1, pair, mid)
+        run("spread", spread, 1, pair, mid)
         send_rows(0, mid, 2 * pair, 2, pair)
-    for frame in range(frames, frames + 2):
-        wsum(1, frame)
-    reduce_core(1)
-
-    fill_frames(0, mid, 2, frames)
-    for pair in range(frames // 2):
-        take_rows(0, mid, 2 * pair, 2, pair)
-    reduce_cross(1)
-    for frame in range(frames):
-        wsum(0, frame)
-    reduce_slots(1)
-    take_late(0, mid)
-    for frame in range(frames, frames + 2):
-        wsum(0, frame)
-    reduce_core(0)
-    reduce_bands(1)
-    spread(0, 0, out_ref)
-    reduce_cross(0)
+    for frame in late_frames:
+        run("wsum", wsum, 1, frame, (0, 2))
+    for group in range(len(groups)):
+        run("red_core", reduce_core, 1, group)
+    run("fill", fill_frames, 0, mid, 2, frames)
+
+    for frame in range(2, frames):
+        run("wsum", wsum, 0, frame, (1,))
     for pair in range(1, frames // 2):
-        spread(0, pair, out_ref)
-    finish(1, grad_second_ref)
-    reduce_slots(0)
-    reduce_bands(0)
-    finish(0, grad_first_ref)
+        run("take_rows", take_rows, 0, mid, 2 * pair, 2, pair)
+    for group in range(len(groups)):
+        run("red_cross", reduce_cross, 1, group)
+    for frame in range(2, frames):
+        run("wsum", wsum, 0, frame, (0, 2))
+    if len(groups) > 1:
+        run("red_core", reduce_core, 0, 1)
+    run("fwd_late", forward_late, 0, mid)
+    for frame in late_frames:
+        run("wsum", wsum, 0, frame, (1,))
+    if len(groups) > 1:
+        run("red_cross", reduce_cross, 0, 1)
+    run("spread", spread, 0, 0, out_ref, zero, zero + 1)
+    run("edges", take_edges, 0)
+    for frame in late_frames:
+        run("wsum", wsum, 0, frame, (0, 2))
+    run("red_core", reduce_core, 0, 0)
+    for part in range(len(parts)):
+        run("red_slots", reduce_slots, 1, part)
+    run("spread", spread, 0, 0, out_ref, zero + 1, zero + chunks)
+    run("red_cross", reduce_cross, 0, 0)
+    for pair in range(1, frames // 2):
+        run("spread", spread, 0, pair, out_ref)
+    for part in range(len(parts)):
+        run("red_slots", reduce_slots, 0, part)
+    for part in range(len(parts)):
+        run("red_bands", reduce_bands, 1, part)
+    run("finish", finish, 1, grad_second_ref)
+    for part in range(len(parts)):
+        run("red_bands", reduce_bands, 0, part)
+    run("finish", finish, 0, grad_first_ref)
 
     def sent(*copies):
         for copy in copies:
@@ -339,10 +401,21 @@
     for flag, copy in ((has_above, edge_up), (has_below, edge_down)):
         when(jnp.logical_and(has_later, flag), lambda copy=copy: sent(*[copy(layer, f) for layer in range(2) for f in range(2)]))
     for layer in range(2):
-        sent(core_copy(layer))
-        sent(*[cross_copy(layer, step) for step in range(1, lanes)])
-        sent(*[slot_copy(layer, step) for step in range(1, slots)])
-        sent(*[band_copy(layer, step) for step in range(1, bands)])
+        for group in range(len(groups)):
+            sent(core_copy(layer, group))
+            sent(*[cross_copy(layer, group, part, step) for part in range(len(parts)) for step in range(1, lanes)])
+        for part in range(len(parts)):
+            sent(*[slot_copy(layer, part, step) for step in range(1, slots)])
+            sent(*[band_copy(layer, part, step) for step in range(1, bands)])
+
+
+def store_kernel(*refs):
+    sources, targets, sems = refs[:3], refs[3:6], refs[6]
+    copies = [pltpu.make_async_copy(src, dst, sems.at[i]) for i, (src, dst) in enumerate(zip(sources, targets))]
+    for copy in copies:
+        copy.start()
+    for copy in copies:
+        copy.wait()
 
 
 def body(upstream, saved_first, saved_second, weight_first, weight_second):
@@ -374,30 +447,35 @@
         vmem((2, slots, chunk, chans), F32),
         vmem((2, slots, chunk, chans), wire),
         vmem((2, slots - 1, chunk, chans), wire),
-        vmem((2, chunk, chans), F32),
-        vmem((2, bands - 1, chunk, chans), F32),
+        vmem((2, bands, chunk, chans), wire),
         dma((5,)),
         dma((2, pairs, 2)), dma((2, pairs, 2)),
         dma((2, 2)), dma((2, 2)),
         dma((2, 2, 2)), dma((2, 2, 2)),
-        dma((2,)), dma((2,)),
-        dma((2, max(1, lanes - 1))), dma((2, max(1, lanes - 1))),
-        dma((2, slots - 1)), dma((2, slots - 1)),
-        dma((2, bands - 1)), dma((2, bands - 1)),
+        dma((2, 2)), dma((2, 2)),
+        dma((2, 2, 2, max(1, lanes - 1))), dma((2, 2, 2, max(1, lanes - 1))),
+        dma((2, 2, slots - 1)), dma((2, 2, slots - 1)),
+        dma((2, 2, bands - 1)), dma((2, 2, bands - 1)),
     ]
-    return pl.pallas_call(
+    shapes = [(upstream.shape, BF16), ((share, chans), F32), ((share, chans), F32)]
+    results = pl.pallas_call(
         functools.partial(whole_kernel, slots, bands, factor),
-        out_shape=[
-            jax.ShapeDtypeStruct(upstream.shape, BF16),
-            jax.ShapeDtypeStruct((share, chans), F32),
-            jax.ShapeDtypeStruct((share, chans), F32),
-        ],
+        out_shape=[pltpu.VMEM(shape, kind) for shape, kind in shapes],
         in_specs=[pl.BlockSpec(memory_space=pl.ANY)] * 5,
         out_specs=[pl.BlockSpec(memory_space=pltpu.VMEM)] * 3,
         scratch_shapes=scratch,
         compiler_params=pltpu.CompilerParams(vmem_limit_bytes=VMEM_LIMIT, collective_id=0, has_side_effects=True),
         name="whole",
     )(upstream, saved_first, saved_second, weight_first, weight_second)
+    return pl.pallas_call(
+        store_kernel,
+        out_shape=[jax.ShapeDtypeStruct(shape, kind) for shape, kind in shapes],
+        in_specs=[pl.BlockSpec(memory_space=pltpu.VMEM)] * 3,
+        out_specs=[pl.BlockSpec(memory_space=pl.ANY)] * 3,
+        scratch_shapes=[dma((3,))],
+        compiler_params=pltpu.CompilerParams(vmem_limit_bytes=2 * 1024 * 1024),
+        name="store",
+    )(*results)
 
 
 def solution(mesh):

time: 64.7 us -> 54.3 us (0.84)
  Pallas kernels: 59.5 us -> 53.3 us
  local copies, waits for them, and re-layouts: 4.05 us -> 0 us
    pallas_call x1, Pallas kernels: 59.5 us -> 52.2 us  [body(): pl.pallas_call(functools.partial(whole_kernel, slots, bands, factor), out...]
    unnamed x7 -> x0, local copies, waits for them, and re-layouts: 4.05 us -> none
    pallas_call x0 -> x1, Pallas kernels: none -> 1.13 us  [body(): pl.pallas_call(store_kernel, out_shape=[jax.ShapeDtypeStruct(shape, kind)...]
where the time goes in v2:
time: 54.3 us; the launch traced here: 54.1 us
  Pallas kernels  53.3 us (98%)
  between operations  0.8 us (1%)
    pallas_call x1, Pallas kernels, body(): pl.pallas_call(functools.partial(whole_kernel, slots, bands, factor), out...  52.2 us
    pallas_call x1, Pallas kernels, body(): pl.pallas_call(store_kernel, out_shape=[jax.ShapeDtypeStruct(shape, kind)...  1.13 us

profile of v2, /device:TPU:0, one launch (start us, length us, event | category | flops | bytes accessed | tf_op | source)
XLA Modules:
  0.0 54.1 jit_solution(13251922256647565023)
XLA Ops:
  0.6 52.2 %whole.1 = (bf16[4,8,128,128]{3,2,1,0:T(8,128)(2,1)S(1)}, f32[432,128]{1,0:T(8,128)S(1)}, f32[432,128]{1,0:T(8,128)S(1)}) custom-call(bf16[4,8,128,128]{3,2,1,0:T(8,128)(2,1)} %up_hbm.1, bf16[4,8,128,128]{3,2,1,0:T(8,128)(2,1)} %first_hbm.1, bf16[4,8,128,128]{3,2,1,0:T(8,128)(2,1)} %second_hbm.1, bf16[3456,128]{1,0:T(8,128)(2,1)} %weight_first_hbm.1, ...), custom_call_target="tpu_custom_call" | custom-call | tf_op jit(solution)/shard_map/whole/pallas_call | solution.py:461
  52.8 1.1 %store.1 = (bf16[4,8,128,128]{3,2,1,0:T(8,128)(2,1)}, f32[432,128]{1,0:T(8,128)}, f32[432,128]{1,0:T(8,128)}) custom-call(bf16[4,8,128,128]{3,2,1,0:T(8,128)(2,1)S(1)} %get-tuple-element.6.refs_0_, f32[432,128]{1,0:T(8,128)S(1)} %get-tuple-element.7.refs_1_, f32[432,128]{1,0:T(8,128)S(1)} %get-tuple-element.8.refs_2_), custom_call_target="tpu_custom_call" | custom-call | tf_op jit(solution)/shard_map/store/pallas_call | solution.py:470

commit v3 on v2

--- a/solution.py
+++ b/solution.py
@@ -25,9 +25,9 @@
     slots, bands, factor,
     up_hbm, first_hbm, second_hbm, weight_first_hbm, weight_second_hbm,
     out_ref, grad_first_ref, grad_second_ref,
-    up, saved, weights, mid, wide, above, below, later, later_above, later_below, kernels, active, total,
+    up, saved, weights, mid, wide, above, below, later, later_above, later_below, saved_above, saved_below, kernels, active, reach, total,
     core_out, core_in, cross_out, cross_in, slot_sum, slot_out, slot_in, band_in,
-    load_sem, row_send, row_recv, late_send, late_recv, edge_send, edge_recv,
+    load_sem, row_send, row_recv, late_send, late_recv, edge_send, edge_recv, seen_send, seen_recv,
     core_send, core_recv, cross_send, cross_recv, slot_send, slot_recv, band_send, band_recv,
 ):
     frames, height, width, chans = up.shape
@@ -77,6 +77,14 @@
     def edge_down(layer, frame):
         return remote(later.at[layer, frame, height - 1], later_above.at[layer, frame], edge_send.at[layer, frame, 1], edge_recv.at[layer, frame, 1], (t, r + 1))
 
+    def seen_up():
+        rows = saved.at[0, pl.ds(frames - 2, 2), 0]
+        return remote(rows, saved_below, seen_send.at[0], seen_recv.at[0], (t, r - 1))
+
+    def seen_down():
+        rows = saved.at[0, pl.ds(frames - 2, 2), height - 1]
+        return remote(rows, saved_above, seen_send.at[1], seen_recv.at[1], (t, r + 1))
+
     def when(flag, *actions):
         @pl.when(flag)
         def _():
@@ -172,16 +180,38 @@
                     )
                     kernels[layer, pl.ds(half * chans, chans), pl.ds(j * span + tap * chans, chans)] = block
 
+    def silu(value):
+        value = value.astype(F32)
+        return value * jax.nn.sigmoid(value)
+
     def make_active(layer):
         def one(frame, carry):
             for row in range(height):
-                value = saved[layer, frame, row].astype(F32)
-                act = value * jax.nn.sigmoid(value)
                 lines = pl.ds(pl.multiple_of(frame * chans, chans), chans)
-                active[layer, lines, pl.ds(row * width, width)] = act.T.astype(BF16)
+                active[layer, lines, pl.ds(row * width, width)] = silu(saved[layer, frame, row]).T.astype(BF16)
             return carry
 
         lax.fori_loop(0, frames, one, 0)
+
+    def send_seen():
+        when(has_above, lambda: seen_up().start())
+        when(has_below, lambda: seen_down().start())
+
+    def make_reach():
+        reach[:, pl.ds(width, height * width)] = active[0, pl.ds((frames - 2) * chans, 2 * chans), :]
+
+        def take(copy, rows, base):
+            copy().wait_recv()
+            for frame in range(2):
+                reach[pl.ds(frame * chans, chans), pl.ds(base, width)] = silu(rows[frame]).T.astype(BF16)
+
+        def clear(base):
+            reach[:, pl.ds(base, width)] = jnp.zeros((2 * chans, width), BF16)
+
+        when(has_above, lambda: take(seen_down, saved_above, 0))
+        when(has_below, lambda: take(seen_up, saved_below, (height + 1) * width))
+        when(jnp.logical_not(has_above), lambda: clear(0))
+        when(jnp.logical_not(has_below), lambda: clear((height + 1) * width))
 
     step_rows = math.gcd(4, height)
     lines = step_rows * width
@@ -219,6 +249,18 @@
                 block = sums[(s - low) * chans : (s - low + 1) * chans, i * chans : (i + 1) * chans]
                 total[layer, rows, :] = block if s == 0 else total[layer, rows, :] + block
 
+    def wsum_late(frame):
+        count = frames + 2 - frame
+        acts = pl.ds((2 - count) * chans, count * chans)
+        lhs = jnp.concatenate([reach[acts, pl.ds(q * width, height * width)] for q in range(3)], axis=0)
+        sums = jnp.dot(lhs, wide[0, frame, pl.ds(width, height * width), :], preferred_element_type=F32)
+        for q in range(3):
+            for i in range(count):
+                p = frames - count + i + 2 - frame
+                for k in range(3):
+                    rows = pl.ds((9 * p + 3 * q + k) * chans, chans)
+                    total[0, rows, :] += sums[(q * count + i) * chans : (q * count + i + 1) * chans, k * chans : (k + 1) * chans]
+
     half_at = lambda which: which * (share - half_rows)
     aligned = lambda value: pl.multiple_of(value, unit)
     settled = min(slots, -(-18 * chans // share))
@@ -251,15 +293,17 @@
             cross_send.at[layer, group, part, step - 1], cross_recv.at[layer, group, part, step - 1], (t, 2 * to + core),
         )
 
-    def reduce_cross(layer, group):
-        core_copy(layer, group).wait_recv()
+    def reduce_cross(layer, group, part):
+        if part == 0:
+            core_copy(layer, group).wait_recv()
+        line, count = parts[part]
         for slot in range(*groups[group]):
-            cross_out[layer, slot] = (
-                total[layer, pl.ds(own_half(slot), half_rows), :] + core_in[layer, slot].astype(F32)
-            ).astype(wire)
-        for part in range(len(parts)):
-            for step in range(1, lanes):
-                cross_copy(layer, group, part, step).start()
+            for to in range(lanes):
+                lines = pl.ds(to * chunk + line, count)
+                value = total[layer, pl.ds(aligned(own_half(slot) + to * chunk + line), count), :]
+                cross_out[layer, slot, lines] = (value + core_in[layer, slot, lines].astype(F32)).astype(wire)
+        for step in range(1, lanes):
+            cross_copy(layer, group, part, step).start()
 
     def slot_copy(layer, part, step):
         to = lax.rem(t + step, slots)
@@ -321,6 +365,13 @@
 
     zero = r // bands
 
+    every_part = range(len(parts))
+    late_group, settled_group = 0, (1 if len(groups) > 1 else None)
+
+    def cross_all(layer, group):
+        for part in every_part:
+            reduce_cross(layer, group, part)
+
     send_rows(1, up, 0, frames, 0)
     send_late(1, up)
     run("fill", fill_frames, 1, up, 0, frames)
@@ -329,6 +380,7 @@
     loads[2].wait()
     run("active", make_active, 1)
     loads[3].wait()
+    send_seen()
     run("active", make_active, 0)
     loads[4].wait()
     run("kernels", make_kernels, 0)
@@ -339,56 +391,59 @@
     run("fill", fill_frames, 0, mid, 0, 2)
     for frame in range(frames - 1):
         run("wsum", wsum, 1, frame)
+    run("reach", make_reach)
     run("take_rows", take_rows, 0, mid, 0, 2, 0)
     for frame in range(2):
         run("wsum", wsum, 0, frame)
     run("fwd_late", forward_late, 1, up)
     run("wsum", wsum, 1, frames - 1)
+    if settled_group:
+        run("red_core", reduce_core, 1, settled_group)
     for frame in late_frames:
         run("wsum", wsum, 1, frame, (1,))
     run("edges", take_edges, 1)
     for pair in range(1, frames // 2):
         run("spread", spread, 1, pair, mid)
         send_rows(0, mid, 2 * pair, 2, pair)
+    if settled_group:
+        run("red_cross", cross_all, 1, settled_group)
     for frame in late_frames:
         run("wsum", wsum, 1, frame, (0, 2))
-    for group in range(len(groups)):
-        run("red_core", reduce_core, 1, group)
+    run("red_core", reduce_core, 1, late_group)
     run("fill", fill_frames, 0, mid, 2, frames)
 
     for frame in range(2, frames):
         run("wsum", wsum, 0, frame, (1,))
+    run("red_cross", cross_all, 1, late_group)
     for pair in range(1, frames // 2):
         run("take_rows", take_rows, 0, mid, 2 * pair, 2, pair)
-    for group in range(len(groups)):
-        run("red_cross", reduce_cross, 1, group)
     for frame in range(2, frames):
         run("wsum", wsum, 0, frame, (0, 2))
-    if len(groups) > 1:
-        run("red_core", reduce_core, 0, 1)
+    if settled_group:
+        run("red_core", reduce_core, 0, settled_group)
     run("fwd_late", forward_late, 0, mid)
     for frame in late_frames:
-        run("wsum", wsum, 0, frame, (1,))
-    if len(groups) > 1:
-        run("red_cross", reduce_cross, 0, 1)
+        run("wsum_late", wsum_late, frame)
+    run("red_core", reduce_core, 0, late_group)
+    if settled_group:
+        run("red_cross", cross_all, 0, settled_group)
+    for part in every_part:
+        run("red_slots", reduce_slots, 1, part)
     run("spread", spread, 0, 0, out_ref, zero, zero + 1)
+    run("red_cross", cross_all, 0, late_group)
+    run("spread", spread, 0, 0, out_ref, zero + 1, zero + chunks)
     run("edges", take_edges, 0)
-    for frame in late_frames:
-        run("wsum", wsum, 0, frame, (0, 2))
-    run("red_core", reduce_core, 0, 0)
-    for part in range(len(parts)):
-        run("red_slots", reduce_slots, 1, part)
-    run("spread", spread, 0, 0, out_ref, zero + 1, zero + chunks)
-    run("red_cross", reduce_cross, 0, 0)
     for pair in range(1, frames // 2):
-        run("spread", spread, 0, pair, out_ref)
-    for part in range(len(parts)):
+        run("spread", spread, 0, pair, out_ref, zero, zero + 1)
+        run("red_slots", reduce_slots, 0, 0)
+        run("spread", spread, 0, pair, out_ref, zero + 1, zero + chunks)
+    for part in every_part[1:]:
         run("red_slots", reduce_slots, 0, part)
-    for part in range(len(parts)):
-        run("red_bands", reduce_bands, 1, part)
-    run("finish", finish, 1, grad_second_ref)
-    for part in range(len(parts)):
+    for part in every_part:
+        run("red_bands_b", reduce_bands, 1, part)
+    for part in every_part:
         run("red_bands", reduce_bands, 0, part)
+    run("finish_b", finish, 1, grad_second_ref)
     run("finish", finish, 0, grad_first_ref)
 
     def sent(*copies):
@@ -398,6 +453,8 @@
     when(has_above, lambda: sent(row_up(1, up, 0, frames, 0), *[row_up(0, mid, 2 * p, 2, p) for p in range(frames // 2)]))
     when(has_below, lambda: sent(row_down(1, up, 0, frames, 0), *[row_down(0, mid, 2 * p, 2, p) for p in range(frames // 2)]))
     when(has_prev, lambda: sent(*[late(1, up, f) for f in range(2)], *[late(0, mid, f) for f in range(2)]))
+    when(has_above, lambda: sent(seen_up()))
+    when(has_below, lambda: sent(seen_down()))
     for flag, copy in ((has_above, edge_up), (has_below, edge_down)):
         when(jnp.logical_and(has_later, flag), lambda copy=copy: sent(*[copy(layer, f) for layer in range(2) for f in range(2)]))
     for layer in range(2):
@@ -437,8 +494,11 @@
         vmem((2, 2, height, width, chans), BF16),
         vmem((2, 2, width, chans), BF16),
         vmem((2, 2, width, chans), BF16),
+        vmem((2, width, chans), BF16),
+        vmem((2, width, chans), BF16),
         vmem((2, 2 * chans, 36 * chans), BF16),
         vmem((2, frames * chans, height * width), BF16),
+        vmem((2 * chans, (height + 2) * width), BF16),
         vmem((2, depth, chans), F32),
         vmem((2, slots, half_rows, chans), wire),
         vmem((2, slots, half_rows, chans), wire),
@@ -452,6 +512,7 @@
         dma((2, pairs, 2)), dma((2, pairs, 2)),
         dma((2, 2)), dma((2, 2)),
         dma((2, 2, 2)), dma((2, 2, 2)),
+        dma((2,)), dma((2,)),
         dma((2, 2)), dma((2, 2)),
         dma((2, 2, 2, max(1, lanes - 1))), dma((2, 2, 2, max(1, lanes - 1))),
         dma((2, 2, slots - 1)), dma((2, 2, slots - 1)),

time: 54.3 us -> 50.7 us (0.934)
  Pallas kernels: 53.3 us -> 49.7 us
    pallas_call x1, Pallas kernels: 52.2 us -> 48.6 us  [body(): pl.pallas_call(functools.partial(whole_kernel, slots, bands, factor), out...]
where the time goes in v3:
time: 50.7 us; the launch traced here: 50.5 us
  Pallas kernels  49.7 us (98%)
  between operations  0.8 us (2%)
    pallas_call x1, Pallas kernels, body(): pl.pallas_call(functools.partial(whole_kernel, slots, bands, factor), out...  48.6 us
    pallas_call x1, Pallas kernels, body(): pl.pallas_call(store_kernel, out_shape=[jax.ShapeDtypeStruct(shape, kind)...  1.13 us

profile of v3, /device:TPU:0, one launch (start us, length us, event | category | flops | bytes accessed | tf_op | source)
XLA Modules:
  0.0 50.5 jit_solution(5208135562436504856)
XLA Ops:
  0.6 48.6 %whole.1 = (bf16[4,8,128,128]{3,2,1,0:T(8,128)(2,1)S(1)}, f32[432,128]{1,0:T(8,128)S(1)}, f32[432,128]{1,0:T(8,128)S(1)}) custom-call(bf16[4,8,128,128]{3,2,1,0:T(8,128)(2,1)} %up_hbm.1, bf16[4,8,128,128]{3,2,1,0:T(8,128)(2,1)} %first_hbm.1, bf16[4,8,128,128]{3,2,1,0:T(8,128)(2,1)} %second_hbm.1, bf16[3456,128]{1,0:T(8,128)(2,1)} %weight_first_hbm.1, ...), custom_call_target="tpu_custom_call" | custom-call | tf_op jit(solution)/shard_map/whole/pallas_call | solution.py:522
  49.2 1.1 %store.1 = (bf16[4,8,128,128]{3,2,1,0:T(8,128)(2,1)}, f32[432,128]{1,0:T(8,128)}, f32[432,128]{1,0:T(8,128)}) custom-call(bf16[4,8,128,128]{3,2,1,0:T(8,128)(2,1)S(1)} %get-tuple-element.6.refs_0_, f32[432,128]{1,0:T(8,128)S(1)} %get-tuple-element.7.refs_1_, f32[432,128]{1,0:T(8,128)S(1)} %get-tuple-element.8.refs_2_), custom_call_target="tpu_custom_call" | custom-call | tf_op jit(solution)/shard_map/store/pallas_call | solution.py:531

commit v4 on v3

--- a/solution.py
+++ b/solution.py
@@ -10,6 +10,7 @@
 
 F32, BF16 = jnp.float32, jnp.bfloat16
 VMEM_LIMIT = 52 * 1024 * 1024
+PARTS = 2
 MESH = pl.DeviceIdType.MESH
 
 
@@ -77,13 +78,13 @@
     def edge_down(layer, frame):
         return remote(later.at[layer, frame, height - 1], later_above.at[layer, frame], edge_send.at[layer, frame, 1], edge_recv.at[layer, frame, 1], (t, r + 1))
 
-    def seen_up():
-        rows = saved.at[0, pl.ds(frames - 2, 2), 0]
-        return remote(rows, saved_below, seen_send.at[0], seen_recv.at[0], (t, r - 1))
-
-    def seen_down():
-        rows = saved.at[0, pl.ds(frames - 2, 2), height - 1]
-        return remote(rows, saved_above, seen_send.at[1], seen_recv.at[1], (t, r + 1))
+    def seen_up(layer):
+        rows = saved.at[layer, pl.ds(frames - 2, 2), 0]
+        return remote(rows, saved_below.at[layer], seen_send.at[layer, 0], seen_recv.at[layer, 0], (t, r - 1))
+
+    def seen_down(layer):
+        rows = saved.at[layer, pl.ds(frames - 2, 2), height - 1]
+        return remote(rows, saved_above.at[layer], seen_send.at[layer, 1], seen_recv.at[layer, 1], (t, r + 1))
 
     def when(flag, *actions):
         @pl.when(flag)
@@ -136,19 +137,18 @@
         when(jnp.logical_not(has_above), *[lambda f=f: zero_row(layer, f, 0) for f in range(low, low + count)])
         when(jnp.logical_not(has_below), *[lambda f=f: zero_row(layer, f, height + 1) for f in range(low, low + count)])
 
-    def forward_late(layer, grad):
-        def forward(frame):
+    def forward_late(layer, grad, frame):
+        def forward():
             late(layer, grad, frame).wait_recv()
             when(has_above, lambda: edge_up(layer, frame).start())
             when(has_below, lambda: edge_down(layer, frame).start())
             fill_frames(layer, later.at[layer], frames + frame, frames + frame + 1, base=frames)
 
-        when(has_later, *[lambda f=f: forward(f) for f in range(2)])
-
-        @pl.when(jnp.logical_not(has_later))
-        def _():
-            for frame in range(2):
-                wide[layer, frames + frame] = jnp.zeros(wide.shape[2:], BF16)
+        def clear():
+            wide[layer, frames + frame] = jnp.zeros(wide.shape[2:], BF16)
+
+        when(has_later, forward)
+        when(jnp.logical_not(has_later), clear)
 
     def take_edges(layer):
         def edges(frame):
@@ -193,20 +193,20 @@
 
         lax.fori_loop(0, frames, one, 0)
 
-    def send_seen():
-        when(has_above, lambda: seen_up().start())
-        when(has_below, lambda: seen_down().start())
-
-    def make_reach():
-        reach[:, pl.ds(width, height * width)] = active[0, pl.ds((frames - 2) * chans, 2 * chans), :]
+    def send_seen(layer):
+        when(has_above, lambda: seen_up(layer).start())
+        when(has_below, lambda: seen_down(layer).start())
+
+    def make_reach(layer):
+        reach[layer, :, pl.ds(width, height * width)] = active[layer, pl.ds((frames - 2) * chans, 2 * chans), :]
 
         def take(copy, rows, base):
-            copy().wait_recv()
+            copy(layer).wait_recv()
             for frame in range(2):
-                reach[pl.ds(frame * chans, chans), pl.ds(base, width)] = silu(rows[frame]).T.astype(BF16)
+                reach[layer, pl.ds(frame * chans, chans), pl.ds(base, width)] = silu(rows[layer, frame]).T.astype(BF16)
 
         def clear(base):
-            reach[:, pl.ds(base, width)] = jnp.zeros((2 * chans, width), BF16)
+            reach[layer, :, pl.ds(base, width)] = jnp.zeros((2 * chans, width), BF16)
 
         when(has_above, lambda: take(seen_down, saved_above, 0))
         when(has_below, lambda: take(seen_up, saved_below, (height + 1) * width))
@@ -246,27 +246,27 @@
             p = s + 2 - frame
             for i, tap in enumerate(3 * q + k for q in taps for k in range(3)):
                 rows = pl.ds((9 * p + tap) * chans, chans)
-                block = sums[(s - low) * chans : (s - low + 1) * chans, i * chans : (i + 1) * chans]
-                total[layer, rows, :] = block if s == 0 else total[layer, rows, :] + block
-
-    def wsum_late(frame):
-        count = frames + 2 - frame
-        acts = pl.ds((2 - count) * chans, count * chans)
-        lhs = jnp.concatenate([reach[acts, pl.ds(q * width, height * width)] for q in range(3)], axis=0)
-        sums = jnp.dot(lhs, wide[0, frame, pl.ds(width, height * width), :], preferred_element_type=F32)
+                total[layer, rows, :] += sums[(s - low) * chans : (s - low + 1) * chans, i * chans : (i + 1) * chans]
+
+    def wsum_late(layer, index):
+        count = 2 - index
+        acts = pl.ds(index * chans, count * chans)
+        lhs = jnp.concatenate([reach[layer, acts, pl.ds(q * width, height * width)] for q in range(3)], axis=0)
+        sums = jnp.dot(lhs, wide[layer, frames + index, pl.ds(width, height * width), :], preferred_element_type=F32)
         for q in range(3):
-            for i in range(count):
-                p = frames - count + i + 2 - frame
+            for p in range(count):
                 for k in range(3):
                     rows = pl.ds((9 * p + 3 * q + k) * chans, chans)
-                    total[0, rows, :] += sums[(q * count + i) * chans : (q * count + i + 1) * chans, k * chans : (k + 1) * chans]
+                    line = (q * count + p) * chans
+                    total[layer, rows, :] += sums[line : line + chans, k * chans : (k + 1) * chans]
 
     half_at = lambda which: which * (share - half_rows)
     aligned = lambda value: pl.multiple_of(value, unit)
-    settled = min(slots, -(-18 * chans // share))
+    settled = min(slots, -(-9 * chans // share))
     groups = [(low, high) for low, high in ((0, settled), (settled, slots)) if low < high]
-    first_rows = -(-chunk // (2 * unit)) * unit
-    parts = [(low, count) for low, count in ((0, first_rows), (first_rows, chunk - first_rows)) if count > 0]
+    units = chunk // unit
+    cuts = [units * i // PARTS * unit for i in range(PARTS + 1)]
+    parts = [(low, high - low) for low, high in zip(cuts, cuts[1:]) if low < high]
     own_half = lambda slot: aligned(slot * share + half_at(core))
 
     def core_copy(layer, group):
@@ -313,12 +313,12 @@
             slot_send.at[layer, part, step - 1], slot_recv.at[layer, part, step - 1], (to, r),
         )
 
-    def reduce_slots(layer, part):
+    def reduce_slots(layer, group, part):
         line, count = parts[part]
-        for group in range(len(groups)):
-            for step in range(1, lanes):
-                cross_copy(layer, group, part, step).wait_recv()
-        for slot in range(slots):
+        low, high = groups[group]
+        for step in range(1, lanes):
+            cross_copy(layer, group, part, step).wait_recv()
+        for slot in range(low, high):
             mine = aligned(lane * chunk + line)
             value = total[layer, pl.ds(aligned(own_half(slot) + mine), count), :]
             value = value + core_in[layer, slot, pl.ds(mine, count), :].astype(F32)
@@ -327,7 +327,8 @@
             slot_sum[layer, slot, pl.ds(line, count), :] = value
             slot_out[layer, slot, pl.ds(line, count), :] = value.astype(wire)
         for step in range(1, slots):
-            slot_copy(layer, part, step).start()
+            to = lax.rem(t + step, slots)
+            when(jnp.logical_and(to >= low, to < high), lambda step=step: slot_copy(layer, part, step).start())
 
     def band_copy(layer, part, step):
         to = lax.rem(r + step, bands)
@@ -361,7 +362,6 @@
             action(*args)
 
     chunks = height // step_rows
-    late_frames = range(frames, frames + 2)
 
     zero = r // bands
 
@@ -371,6 +371,14 @@
     def cross_all(layer, group):
         for part in every_part:
             reduce_cross(layer, group, part)
+
+    def clear_total():
+        def one(index, carry):
+            for layer in range(2):
+                total[layer, pl.ds(pl.multiple_of(index * chans, chans), chans), :] = jnp.zeros((chans, chans), F32)
+            return carry
+
+        lax.fori_loop(0, 27, one, 0)
 
     send_rows(1, up, 0, frames, 0)
     send_late(1, up)
@@ -378,67 +386,73 @@
     loads[1].wait()
     run("kernels", make_kernels, 1)
     loads[2].wait()
+    send_seen(1)
     run("active", make_active, 1)
     loads[3].wait()
-    send_seen()
+    send_seen(0)
     run("active", make_active, 0)
     loads[4].wait()
-    run("kernels", make_kernels, 0)
+    run("clear", clear_total)
     run("take_rows", take_rows, 1, up, 0, frames, 0)
     run("spread", spread, 1, 0, mid)
     send_rows(0, mid, 0, 2, 0)
     send_late(0, mid)
     run("fill", fill_frames, 0, mid, 0, 2)
-    for frame in range(frames - 1):
+    run("kernels", make_kernels, 0)
+    for frame in range(frames):
         run("wsum", wsum, 1, frame)
-    run("reach", make_reach)
+    run("reach", make_reach, 1)
+    run("reach", make_reach, 0)
+    run("fwd_late", forward_late, 1, up, 0)
+    run("wsum_late", wsum_late, 1, 0)
+    if settled_group:
+        run("red_core", reduce_core, 1, settled_group)
+    run("fwd_late", forward_late, 1, up, 1)
+    run("wsum_late", wsum_late, 1, 1)
+    run("red_core", reduce_core, 1, late_group)
     run("take_rows", take_rows, 0, mid, 0, 2, 0)
     for frame in range(2):
         run("wsum", wsum, 0, frame)
-    run("fwd_late", forward_late, 1, up)
-    run("wsum", wsum, 1, frames - 1)
+    run("edges", take_edges, 1)
     if settled_group:
-        run("red_core", reduce_core, 1, settled_group)
-    for frame in late_frames:
-        run("wsum", wsum, 1, frame, (1,))
-    run("edges", take_edges, 1)
+        run("red_cross", cross_all, 1, settled_group)
     for pair in range(1, frames // 2):
         run("spread", spread, 1, pair, mid)
         send_rows(0, mid, 2 * pair, 2, pair)
-    if settled_group:
-        run("red_cross", cross_all, 1, settled_group)
-    for frame in late_frames:
-        run("wsum", wsum, 1, frame, (0, 2))
-    run("red_core", reduce_core, 1, late_group)
+    run("red_cross", cross_all, 1, late_group)
     run("fill", fill_frames, 0, mid, 2, frames)
 
     for frame in range(2, frames):
         run("wsum", wsum, 0, frame, (1,))
-    run("red_cross", cross_all, 1, late_group)
+    run("fwd_late", forward_late, 0, mid, 0)
+    run("wsum_late", wsum_late, 0, 0)
     for pair in range(1, frames // 2):
         run("take_rows", take_rows, 0, mid, 2 * pair, 2, pair)
     for frame in range(2, frames):
         run("wsum", wsum, 0, frame, (0, 2))
     if settled_group:
         run("red_core", reduce_core, 0, settled_group)
-    run("fwd_late", forward_late, 0, mid)
-    for frame in late_frames:
-        run("wsum_late", wsum_late, frame)
+    run("fwd_late", forward_late, 0, mid, 1)
+    run("wsum_late", wsum_late, 0, 1)
     run("red_core", reduce_core, 0, late_group)
     if settled_group:
-        run("red_cross", cross_all, 0, settled_group)
-    for part in every_part:
-        run("red_slots", reduce_slots, 1, part)
+        run("red_cross_s", cross_all, 0, settled_group)
+    for group in range(len(groups)):
+        for part in every_part:
+            run("red_slots_b", reduce_slots, 1, group, part)
     run("spread", spread, 0, 0, out_ref, zero, zero + 1)
-    run("red_cross", cross_all, 0, late_group)
+    run("red_cross_l", cross_all, 0, late_group)
     run("spread", spread, 0, 0, out_ref, zero + 1, zero + chunks)
     run("edges", take_edges, 0)
     for pair in range(1, frames // 2):
         run("spread", spread, 0, pair, out_ref, zero, zero + 1)
-        run("red_slots", reduce_slots, 0, 0)
+    if settled_group:
+        for part in every_part:
+            run("red_slots_s", reduce_slots, 0, settled_group, part)
+    for pair in range(1, frames // 2):
         run("spread", spread, 0, pair, out_ref, zero + 1, zero + chunks)
-    for part in every_part[1:]:
-        run("red_slots", reduce_slots, 0, part)
+    for part in every_part:
+        run("red_slots_l", reduce_slots, 0, late_group, part)
     for part in every_part:
         run("red_bands_b", reduce_bands, 1, part)
     for part in every_part:
@@ -453,8 +467,8 @@
     when(has_above, lambda: sent(row_up(1, up, 0, frames, 0), *[row_up(0, mid, 2 * p, 2, p) for p in range(frames // 2)]))
     when(has_below, lambda: sent(row_down(1, up, 0, frames, 0), *[row_down(0, mid, 2 * p, 2, p) for p in range(frames // 2)]))
     when(has_prev, lambda: sent(*[late(1, up, f) for f in range(2)], *[late(0, mid, f) for f in range(2)]))
-    when(has_above, lambda: sent(seen_up()))
-    when(has_below, lambda: sent(seen_down()))
+    when(has_above, lambda: sent(seen_up(0), seen_up(1)))
+    when(has_below, lambda: sent(seen_down(0), seen_down(1)))
     for flag, copy in ((has_above, edge_up), (has_below, edge_down)):
         when(jnp.logical_and(has_later, flag), lambda copy=copy: sent(*[copy(layer, f) for layer in range(2) for f in range(2)]))
     for layer in range(2):
@@ -494,11 +508,11 @@
         vmem((2, 2, height, width, chans), BF16),
         vmem((2, 2, width, chans), BF16),
         vmem((2, 2, width, chans), BF16),
-        vmem((2, width, chans), BF16),
-        vmem((2, width, chans), BF16),
+        vmem((2, 2, width, chans), BF16),
+        vmem((2, 2, width, chans), BF16),
         vmem((2, 2 * chans, 36 * chans), BF16),
         vmem((2, frames * chans, height * width), BF16),
-        vmem((2 * chans, (height + 2) * width), BF16),
+        vmem((2, 2 * chans, (height + 2) * width), BF16),
         vmem((2, depth, chans), F32),
         vmem((2, slots, half_rows, chans), wire),
         vmem((2, slots, half_rows, chans), wire),
@@ -512,11 +526,11 @@
         dma((2, pairs, 2)), dma((2, pairs, 2)),
         dma((2, 2)), dma((2, 2)),
         dma((2, 2, 2)), dma((2, 2, 2)),
-        dma((2,)), dma((2,)),
         dma((2, 2)), dma((2, 2)),
-        dma((2, 2, 2, max(1, lanes - 1))), dma((2, 2, 2, max(1, lanes - 1))),
-        dma((2, 2, slots - 1)), dma((2, 2, slots - 1)),
-        dma((2, 2, bands - 1)), dma((2, 2, bands - 1)),
+        dma((2, 2)), dma((2, 2)),
+        dma((2, 2, PARTS, max(1, lanes - 1))), dma((2, 2, PARTS, max(1, lanes - 1))),
+        dma((2, PARTS, slots - 1)), dma((2, PARTS, slots - 1)),
+        dma((2, PARTS, bands - 1)), dma((2, PARTS, bands - 1)),
     ]
     shapes = [(upstream.shape, BF16), ((share, chans), F32), ((share, chans), F32)]
     results = pl.pallas_call(

time: 50.7 us -> 50.2 us (level)
  no operation moved by 1% of the time
where the time goes in v4:
time: 50.2 us; the launch traced here: 50 us
  Pallas kernels  49.2 us (98%)
  between operations  0.8 us (2%)
    pallas_call x1, Pallas kernels, body(): pl.pallas_call(functools.partial(whole_kernel, slots, bands, factor), out...  48.1 us
    pallas_call x1, Pallas kernels, body(): pl.pallas_call(store_kernel, out_shape=[jax.ShapeDtypeStruct(shape, kind)...  1.13 us

profile of v4, /device:TPU:0, one launch (start us, length us, event | category | flops | bytes accessed | tf_op | source)
XLA Modules:
  0.0 50.0 jit_solution(14227400868999358012)
XLA Ops:
  0.6 48.1 %whole.1 = (bf16[4,8,128,128]{3,2,1,0:T(8,128)(2,1)S(1)}, f32[432,128]{1,0:T(8,128)S(1)}, f32[432,128]{1,0:T(8,128)S(1)}) custom-call(bf16[4,8,128,128]{3,2,1,0:T(8,128)(2,1)} %up_hbm.1, bf16[4,8,128,128]{3,2,1,0:T(8,128)(2,1)} %first_hbm.1, bf16[4,8,128,128]{3,2,1,0:T(8,128)(2,1)} %second_hbm.1, bf16[3456,128]{1,0:T(8,128)(2,1)} %weight_first_hbm.1, ...), custom_call_target="tpu_custom_call" | custom-call | tf_op jit(solution)/shard_map/whole/pallas_call | solution.py:536
  48.8 1.1 %store.1 = (bf16[4,8,128,128]{3,2,1,0:T(8,128)(2,1)}, f32[432,128]{1,0:T(8,128)}, f32[432,128]{1,0:T(8,128)}) custom-call(bf16[4,8,128,128]{3,2,1,0:T(8,128)(2,1)S(1)} %get-tuple-element.6.refs_0_, f32[432,128]{1,0:T(8,128)S(1)} %get-tuple-element.7.refs_1_, f32[432,128]{1,0:T(8,128)S(1)} %get-tuple-element.8.refs_2_), custom_call_target="tpu_custom_call" | custom-call | tf_op jit(solution)/shard_map/store/pallas_call | solution.py:545

commit v5 on v4

--- a/solution.py
+++ b/solution.py
@@ -10,7 +10,7 @@
 
 F32, BF16 = jnp.float32, jnp.bfloat16
 VMEM_LIMIT = 52 * 1024 * 1024
-PARTS = 2
+PARTS = 1
 MESH = pl.DeviceIdType.MESH
 
 
@@ -79,11 +79,11 @@
         return remote(later.at[layer, frame, height - 1], later_above.at[layer, frame], edge_send.at[layer, frame, 1], edge_recv.at[layer, frame, 1], (t, r + 1))
 
     def seen_up(layer):
-        rows = saved.at[layer, pl.ds(frames - 2, 2), 0]
+        rows = saved.at[layer, :, 0]
         return remote(rows, saved_below.at[layer], seen_send.at[layer, 0], seen_recv.at[layer, 0], (t, r - 1))
 
     def seen_down(layer):
-        rows = saved.at[layer, pl.ds(frames - 2, 2), height - 1]
+        rows = saved.at[layer, :, height - 1]
         return remote(rows, saved_above.at[layer], seen_send.at[layer, 1], seen_recv.at[layer, 1], (t, r + 1))
 
     def when(flag, *actions):
@@ -198,15 +198,15 @@
         when(has_below, lambda: seen_down(layer).start())
 
     def make_reach(layer):
-        reach[layer, :, pl.ds(width, height * width)] = active[layer, pl.ds((frames - 2) * chans, 2 * chans), :]
+        reach[layer, :, pl.ds(width, height * width)] = active[layer]
 
         def take(copy, rows, base):
             copy(layer).wait_recv()
-            for frame in range(2):
+            for frame in range(frames):
                 reach[layer, pl.ds(frame * chans, chans), pl.ds(base, width)] = silu(rows[layer, frame]).T.astype(BF16)
 
         def clear(base):
-            reach[layer, :, pl.ds(base, width)] = jnp.zeros((2 * chans, width), BF16)
+            reach[layer, :, pl.ds(base, width)] = jnp.zeros((frames * chans, width), BF16)
 
         when(has_above, lambda: take(seen_down, saved_above, 0))
         when(has_below, lambda: take(seen_up, saved_below, (height + 1) * width))
@@ -248,16 +248,18 @@
                 rows = pl.ds((9 * p + tap) * chans, chans)
                 total[layer, rows, :] += sums[(s - low) * chans : (s - low + 1) * chans, i * chans : (i + 1) * chans]
 
-    def wsum_late(layer, index):
-        count = 2 - index
-        acts = pl.ds(index * chans, count * chans)
+    def wsum_own(layer, frame):
+        low, high = max(0, frame - 2), min(frames, frame + 1)
+        count = high - low
+        acts = pl.ds(low * chans, count * chans)
         lhs = jnp.concatenate([reach[layer, acts, pl.ds(q * width, height * width)] for q in range(3)], axis=0)
-        sums = jnp.dot(lhs, wide[layer, frames + index, pl.ds(width, height * width), :], preferred_element_type=F32)
+        sums = jnp.dot(lhs, wide[layer, frame, pl.ds(width, height * width), :], preferred_element_type=F32)
         for q in range(3):
-            for p in range(count):
+            for i in range(count):
+                p = low + i + 2 - frame
                 for k in range(3):
                     rows = pl.ds((9 * p + 3 * q + k) * chans, chans)
-                    line = (q * count + p) * chans
+                    line = (q * count + i) * chans
                     total[layer, rows, :] += sums[line : line + chans, k * chans : (k + 1) * chans]
 
     half_at = lambda which: which * (share - half_rows)
@@ -404,11 +406,11 @@
     run("reach", make_reach, 1)
     run("reach", make_reach, 0)
     run("fwd_late", forward_late, 1, up, 0)
-    run("wsum_late", wsum_late, 1, 0)
+    run("wsum_late", wsum_own, 1, frames + 0)
     if settled_group:
         run("red_core", reduce_core, 1, settled_group)
     run("fwd_late", forward_late, 1, up, 1)
-    run("wsum_late", wsum_late, 1, 1)
+    run("wsum_late", wsum_own, 1, frames + 1)
     run("red_core", reduce_core, 1, late_group)
     run("take_rows", take_rows, 0, mid, 0, 2, 0)
     for frame in range(2):
@@ -423,23 +425,21 @@
     run("fill", fill_frames, 0, mid, 2, frames)
 
     for frame in range(2, frames):
-        run("wsum", wsum, 0, frame, (1,))
+        run("wsum_own", wsum_own, 0, frame)
     run("fwd_late", forward_late, 0, mid, 0)
-    run("wsum_late", wsum_late, 0, 0)
-    for pair in range(1, frames // 2):
-        run("take_rows", take_rows, 0, mid, 2 * pair, 2, pair)
-    for frame in range(2, frames):
-        run("wsum", wsum, 0, frame, (0, 2))
+    run("wsum_late", wsum_own, 0, frames + 0)
     if settled_group:
         run("red_core", reduce_core, 0, settled_group)
     run("fwd_late", forward_late, 0, mid, 1)
-    run("wsum_late", wsum_late, 0, 1)
+    run("wsum_late", wsum_own, 0, frames + 1)
     run("red_core", reduce_core, 0, late_group)
     if settled_group:
         run("red_cross_s", cross_all, 0, settled_group)
     for group in range(len(groups)):
         for part in every_part:
             run("red_slots_b", reduce_slots, 1, group, part)
+    for pair in range(1, frames // 2):
+        run("take_rows", take_rows, 0, mid, 2 * pair, 2, pair)
     run("spread", spread, 0, 0, out_ref, zero, zero + 1)
     run("red_cross_l", cross_all, 0, late_group)
     run("spread", spread, 0, 0, out_ref, zero + 1, zero + chunks)
@@ -508,11 +508,11 @@
         vmem((2, 2, height, width, chans), BF16),
         vmem((2, 2, width, chans), BF16),
         vmem((2, 2, width, chans), BF16),
-        vmem((2, 2, width, chans), BF16),
-        vmem((2, 2, width, chans), BF16),
+        vmem((2, frames, width, chans), BF16),
+        vmem((2, frames, width, chans), BF16),
         vmem((2, 2 * chans, 36 * chans), BF16),
         vmem((2, frames * chans, height * width), BF16),
-        vmem((2, 2 * chans, (height + 2) * width), BF16),
+        vmem((2, frames * chans, (height + 2) * width), BF16),
         vmem((2, depth, chans), F32),
         vmem((2, slots, half_rows, chans), wire),
         vmem((2, slots, half_rows, chans), wire),

time: 50.2 us -> 48.6 us (0.968)
  Pallas kernels: 49.2 us -> 47.7 us
    pallas_call x1, Pallas kernels: 48.1 us -> 46.5 us  [body(): pl.pallas_call(functools.partial(whole_kernel, slots, bands, factor), out...]
where the time goes in v5:
time: 48.6 us; the launch traced here: 48.5 us
  Pallas kernels  47.7 us (98%)
  between operations  0.8 us (2%)
    pallas_call x1, Pallas kernels, body(): pl.pallas_call(functools.partial(whole_kernel, slots, bands, factor), out...  46.5 us
    pallas_call x1, Pallas kernels, body(): pl.pallas_call(store_kernel, out_shape=[jax.ShapeDtypeStruct(shape, kind)...  1.13 us

profile of v5, /device:TPU:0, one launch (start us, length us, event | category | flops | bytes accessed | tf_op | source)
XLA Modules:
  0.0 48.5 jit_solution(5839645801009710005)
XLA Ops:
  0.6 46.5 %whole.1 = (bf16[4,8,128,128]{3,2,1,0:T(8,128)(2,1)S(1)}, f32[432,128]{1,0:T(8,128)S(1)}, f32[432,128]{1,0:T(8,128)S(1)}) custom-call(bf16[4,8,128,128]{3,2,1,0:T(8,128)(2,1)} %up_hbm.1, bf16[4,8,128,128]{3,2,1,0:T(8,128)(2,1)} %first_hbm.1, bf16[4,8,128,128]{3,2,1,0:T(8,128)(2,1)} %second_hbm.1, bf16[3456,128]{1,0:T(8,128)(2,1)} %weight_first_hbm.1, ...), custom_call_target="tpu_custom_call" | custom-call | tf_op jit(solution)/shard_map/whole/pallas_call | solution.py:536
  47.2 1.1 %store.1 = (bf16[4,8,128,128]{3,2,1,0:T(8,128)(2,1)}, f32[432,128]{1,0:T(8,128)}, f32[432,128]{1,0:T(8,128)}) custom-call(bf16[4,8,128,128]{3,2,1,0:T(8,128)(2,1)S(1)} %get-tuple-element.6.refs_0_, f32[432,128]{1,0:T(8,128)S(1)} %get-tuple-element.7.refs_1_, f32[432,128]{1,0:T(8,128)S(1)} %get-tuple-element.8.refs_2_), custom_call_target="tpu_custom_call" | custom-call | tf_op jit(solution)/shard_map/store/pallas_call | solution.py:545
